TPU v7x, 32 devices: a whole 2x2x4 slice. The times are simulated.
32 devices in a mesh: cuts: 8 (over y, x, core), grp: 4 (over z).
Axes of the slice: x: 2, y: 2, z: 4, core: 2. Of those that a mesh axis runs over, the one named last changes fastest.
Arguments:
- boundary: float32 [32, 2, 32, 32, 32], P('grp'), may hold values from -12 to 12
- gate_stack: float32 [3, 2, 1024, 1024], P(None, None, 'cuts'), may hold values from -0.125 to 0.125
- layer_order: int32 [3], replicated, may hold values from 0 to 2, each once
- cut_index: int32 [6, 3], replicated, may hold values from 0 to 4, as said below
- slice_bits: int32 [8, 6], P('cuts'), may hold values 0 or 1
- bitstrings: int32 [64, 20], replicated, may hold values 0 or 1
Outputs:
- amplitudes: float32 [64, 2], replicated
Inputs may be any that keep to these rules, and one draw needn't show every extreme that they name: Each row of cut_index is (layer 0 to 2, group 0 to 3, bit 0 to 4); no two rows are equal. Rows of slice_bits need not differ.
All inputs are finite; a program needn't handle non-finite values.
Results may differ from a plain program's by a relative error of at most 0.0003.
Values sent between devices are 32-bit elements.
A program may use at most 320 MiB of HBM per device.

v0:
```python
from functools import partial

import jax
import jax.numpy as jnp
from jax import lax
from jax.sharding import PartitionSpec as P

LAYER_KINDS = (0, 1, 2, 3, 2, 3, 0, 1)
PAIR_GROUPS = ((0, 1), (2, 3), (1, 2), (1, 3))
GROUP_DIMS = (0, 3, 4, 5)
FULL_PRECISION = lax.Precision.HIGHEST


def slice_factors(cut_index, slice_bits, layer_id, group_id, extent, offset):
    positions = offset + jnp.arange(extent, dtype=jnp.int32)
    active = jnp.logical_and(cut_index[:, 0] == layer_id, cut_index[:, 1] == group_id)
    bit_values = jnp.right_shift(positions[:, None], cut_index[None, :, 2]) & 1
    agrees = bit_values[None, :, :] == slice_bits[:, None, :]
    kept = jnp.logical_or(agrees, jnp.logical_not(active)[None, None, :])
    return jnp.all(kept, axis=2).astype(jnp.float32)


def group_digits(bitstrings, group_bits):
    weights = jnp.left_shift(
        jnp.ones((group_bits,), jnp.int32), jnp.arange(group_bits, dtype=jnp.int32)
    )
    return [
        jnp.sum(
            bitstrings[:, group_id * group_bits : (group_id + 1) * group_bits] * weights, axis=1
        ).astype(jnp.int32)
        for group_id in range(4)
    ]


def rotated(current):
    return jnp.concatenate((-current[:, :, 1:2], current[:, :, 0:1]), axis=2)


def local_pair(current, first_dim, second_dim, produce):
    aligned = jnp.moveaxis(current, (first_dim, second_dim), (0, 1))
    turned = jnp.moveaxis(rotated(current), (first_dim, second_dim), (0, 1))
    in_rows = aligned.shape[0] * aligned.shape[1]
    outcome = produce(aligned.reshape(in_rows, -1), turned.reshape(in_rows, -1))
    extent = aligned.shape[1]
    outcome = outcome.reshape((extent, extent) + aligned.shape[2:])
    return jnp.moveaxis(outcome, (0, 1), (first_dim, second_dim))


def body(boundary, gate_stack, layer_order, cut_index, slice_bits, bitstrings):
    member = lax.axis_index("grp")
    gate_source = lax.all_gather(gate_stack, "cuts", axis=2, tiled=True)

    def gate_product(layer_id, direct, swapped, column_start, col_count):

        def rows_from(piece):
            columns = lax.dynamic_slice_in_dim(piece, column_start, col_count, 2)
            return jnp.dot(
                columns[0], direct, precision=FULL_PRECISION, preferred_element_type=jnp.float32
            ) + jnp.dot(
                columns[1], swapped, precision=FULL_PRECISION, preferred_element_type=jnp.float32
            )

        chosen = lax.dynamic_index_in_dim(gate_source, layer_order[layer_id], 0, keepdims=False)
        return rows_from(chosen)

    slice_count = slice_bits.shape[0]
    row_count = boundary.shape[0]
    extent = boundary.shape[2]
    current = jnp.broadcast_to(boundary[:, None], (row_count, slice_count) + boundary.shape[1:])
    for layer_id in range(layer_order.shape[0]):
        first_group, second_group = PAIR_GROUPS[LAYER_KINDS[layer_id % 8]]
        if first_group == 0:
            widened = lax.all_to_all(current, "grp", split_axis=5, concat_axis=0, tiled=True)
            widened = local_pair(
                widened,
                0,
                3,
                partial(gate_product, layer_id, column_start=0, col_count=extent * extent),
            )
            current = lax.all_to_all(widened, "grp", split_axis=0, concat_axis=5, tiled=True)
        else:
            current = local_pair(
                current,
                GROUP_DIMS[first_group],
                GROUP_DIMS[second_group],
                partial(gate_product, layer_id, column_start=0, col_count=extent * extent),
            )
        for group_id in range(4):
            dim_pos = GROUP_DIMS[group_id]
            if group_id == 0:
                factor = slice_factors(
                    cut_index, slice_bits, layer_id, 0, row_count, row_count * member
                ).T
                target_shape = (row_count, slice_count, 1, 1, 1, 1)
            else:
                factor = slice_factors(cut_index, slice_bits, layer_id, group_id, extent, 0)
                target_shape = tuple(
                    (
                        slice_count if position == 1 else extent if position == dim_pos else 1
                        for position in range(6)
                    )
                )
            current = current * factor.reshape(target_shape)
    digits = group_digits(bitstrings, bitstrings.shape[1] // 4)
    summed = jnp.sum(current, axis=1)
    local_row = digits[0] - row_count * member
    inside = jnp.logical_and(local_row >= 0, local_row < row_count)
    picked = summed[jnp.clip(local_row, 0, row_count - 1), :, digits[1], digits[2], digits[3]]
    picked = picked * inside[:, None].astype(jnp.float32)
    return lax.psum(picked, ("cuts", "grp"))


def solution(mesh):
    return jax.shard_map(
        body,
        mesh=mesh,
        in_specs=(
            P("grp", None, None, None, None),
            P(None, None, "cuts", None),
            P(),
            P(),
            P("cuts", None),
            P(),
        ),
        out_specs=P(),
        check_vma=False,
    )
```

profile of v0, /device:TPU:0, one launch (start us, length us, event | category | flops | bytes accessed | tf_op | source)
XLA Modules:
  0.0 552.0 jit_solution(5687589578765140140)
XLA Ops:
  7.3 10.8 %copy.83 = f32[8,2,32,32,32]{3,2,1,0,4:T(8,128)} copy(f32[8,2,32,32,32]{4,3,2,1,0:T(8,128)} %param.6) | data formatting | bytes 4194304 | tf_op args[0]
  18.1 8.5 %bitcast_bitcast_fusion = f32[32,1,8,2,32,32]{5,4,3,2,1,0:T(8,128)} fusion(f32[8,2,32,32,32]{3,2,1,0,4:T(8,128)} %copy.83), kind=kLoop, calls=%fused_computation.100 | loop fusion | bytes 4194304
  26.6 7.1 %reshape.1435 = f32[4,1,131072]{2,1,0:T(1,128)} reshape(f32[32,1,8,2,32,32]{5,4,3,2,1,0:T(8,128)} %bitcast_bitcast_fusion) | data formatting | bytes 4194304
  33.7 6.6 %all-to-all-start = ((f32[4,1,131072]{2,1,0:T(1,128)}), f32[4,1,131072]{2,1,0:T(1,128)S(1)}, u32[]{:S(2)}, u32[]{:S(2)}) async-start(f32[4,1,131072]{2,1,0:T(1,128)} %reshape.1435), calls=%async_computation | async-start | bytes 4194304 | tf_op jit(solution)/shard_map/all_to_all | solution.py:73
  43.0 45.3 %all-to-all-done = f32[4,1,131072]{2,1,0:T(1,128)S(1)} async-done(((f32[4,1,131072]{2,1,0:T(1,128)}), f32[4,1,131072]{2,1,0:T(1,128)S(1)}, u32[]{:S(2)}, u32[]{:S(2)}) %all-to-all-start) | async-done | bytes 2097184 | tf_op jit(solution)/shard_map/all_to_all | solution.py:73
  90.1 7.7 %reduce.12 = f32[4,131072]{1,0:T(4,128)S(1)} reduce(f32[4,1,131072]{2,1,0:T(1,128)} %copy-done.2, f32[]{:T(128)} %broadcast.1202), dimensions={1}, to_apply=%all_to_all.26.reduce_sub_computation | reduce | bytes 4194308 | tf_op jit(solution)/shard_map/all_to_all | solution.py:73
  104.0 10.4 %copy.115 = f32[8,1,2,32,32,32]{4,5,3,2,0,1:T(8,128)S(1)} copy(f32[8,1,2,32,32,32]{4,3,2,0,1,5:T(8,128)} %bitcast.155) | data formatting | bytes 4194304 | tf_op jit(solution)/shard_map/all_to_all | solution.py:73
  122.6 11.6 %copy.87 = f32[32,32,1,2,32,8]{1,0,5,4,3,2:T(8,128)} copy(f32[32,32,1,2,32,8]{4,5,1,3,2,0:T(8,128)} %maximum_bitcast_fusion) | data formatting | bytes 4194304 | tf_op jit(solution)/shard_map/transpose | solution.py:41
  140.9 11.6 %copy.86 = f32[32,32,1,2,32,8]{1,0,5,4,3,2:T(8,128)} copy(f32[32,32,1,2,32,8]{4,5,1,3,2,0:T(8,128)} %bitcast.152) | data formatting | bytes 4194304 | tf_op jit(solution)/shard_map/transpose | solution.py:40
  152.4 7.7 %reshape.1419 = f32[1024,512]{0,1:T(8,128)} reshape(f32[32,32,1,2,32,8]{1,0,5,4,3,2:T(8,128)} %copy.86) | data formatting | bytes 4194304 | tf_op jit(solution)/shard_map/reshape | solution.py:43
  160.1 9.0 %fusion.11 = f32[1024,512]{1,0:T(8,128)S(1)} fusion(f32[1024,512]{0,1:T(8,128)S(1)} %reshape.1420, f32[3,2,1024,1024]{3,2,1,0:T(8,128)} %all-gather.2.cloned.1.call-done, s32[]{:T(128)S(6)} %select_n.52, s32[]{:T(128)S(6)} %add.87), kind=kOutput, calls=%fused_computation.25 | convolution fusion | flops 6442450944 | bytes 8388616 | tf_op jit(solution)/shard_map/dot_general | solution.py:59
  169.1 9.8 %fusion.17 = f32[1024,512]{1,0:T(8,128)} fusion(f32[1024,512]{1,0:T(8,128)S(1)} %fusion.11, f32[1024,512]{0,1:T(8,128)S(1)} %copy-done.3, f32[3,2,1024,1024]{3,2,1,0:T(8,128)} %all-gather.2.cloned.1.call-done, s32[]{:T(128)S(6)} %select_n.52), kind=kOutput, calls=%fused_computation.34 | convolution fusion | flops 6442975232 | bytes 10485764 | tf_op jit(solution)/shard_map/dot_general | solution.py:57
  185.8 11.4 %copy.116 = f32[32,1,2,32,32,8]{3,5,4,2,1,0:T(8,128)} copy(f32[32,1,2,32,32,8]{3,0,5,4,2,1:T(8,128)} %bitcast.156) | data formatting | bytes 4194304 | tf_op jit(solution)/shard_map/transpose | solution.py:46
  197.3 7.1 %reshape.1437 = f32[4,1,131072]{2,1,0:T(1,128)} reshape(f32[32,1,2,32,8,32]{5,4,3,2,1,0:T(8,128)} %bitcast.157) | data formatting | bytes 4194304
  213.7 43.2 %all-to-all-done.1 = f32[4,1,131072]{2,1,0:T(1,128)} async-done(((f32[4,1,131072]{2,1,0:T(1,128)}), f32[4,1,131072]{2,1,0:T(1,128)}, u32[]{:S(2)}, u32[]{:S(2)}) %all-to-all-start.1) | async-done | bytes 2097184 | tf_op jit(solution)/shard_map/all_to_all | solution.py:80
  256.9 7.7 %reduce.13 = f32[4,131072]{1,0:T(4,128)S(1)} reduce(f32[4,1,131072]{2,1,0:T(1,128)} %all-to-all-done.1, f32[]{:T(128)} %broadcast.1202), dimensions={1}, to_apply=%all_to_all.30.reduce_sub_computation | reduce | bytes 4194308 | tf_op jit(solution)/shard_map/all_to_all | solution.py:80
  270.8 9.6 %copy.90 = f32[32,1,2,32,32,8]{4,5,3,2,1,0:T(8,128)} copy(f32[32,1,2,32,32,8]{3,5,4,2,1,0:T(8,128)} %bitcast.158) | data formatting | bytes 4194304 | tf_op jit(solution)/shard_map/all_to_all | solution.py:80
  296.5 9.0 %copy.93 = f32[32,32,8,1,2,32]{1,0,5,4,2,3:T(8,128)} copy(f32[32,32,8,1,2,32]{0,1,5,4,2,3:T(8,128)} %maximum_bitcast_fusion.1) | data formatting | bytes 4194304 | tf_op jit(solution)/shard_map/transpose | solution.py:41
  312.1 9.0 %copy.92 = f32[32,32,8,1,2,32]{1,0,5,4,2,3:T(8,128)} copy(f32[32,32,8,1,2,32]{0,1,5,4,2,3:T(8,128)} %fusion.43) | data formatting | bytes 4194304 | tf_op jit(solution)/shard_map/transpose | solution.py:40
  321.1 7.7 %reshape.1422 = f32[1024,512]{0,1:T(8,128)} reshape(f32[32,32,8,1,2,32]{1,0,5,4,2,3:T(8,128)} %copy.92) | data formatting | bytes 4194304 | tf_op jit(solution)/shard_map/reshape | solution.py:43
  328.8 9.0 %fusion.10 = f32[1024,512]{1,0:T(8,128)S(1)} fusion(f32[1024,512]{0,1:T(8,128)S(1)} %reshape.1423, f32[3,2,1024,1024]{3,2,1,0:T(8,128)} %all-gather.2.cloned.1.call-done, s32[]{:T(128)S(6)} %select_n.51, s32[]{:T(128)S(6)} %add.87), kind=kOutput, calls=%fused_computation.22 | convolution fusion | flops 6442450944 | bytes 8388616 | tf_op jit(solution)/shard_map/dot_general | solution.py:59
  337.8 8.8 %fusion.16 = f32[1024,512]{1,0:T(8,128)S(1)} fusion(f32[1024,512]{1,0:T(8,128)S(1)} %fusion.10, f32[1024,512]{0,1:T(8,128)S(1)} %copy-done.5, f32[3,2,1024,1024]{3,2,1,0:T(8,128)} %all-gather.2.cloned.1.call-done, s32[]{:T(128)S(6)} %select_n.51), kind=kOutput, calls=%fused_computation.33 | convolution fusion | flops 6442975232 | bytes 10485764 | tf_op jit(solution)/shard_map/dot_general | solution.py:57
  346.6 8.3 %reshape.1424 = f32[32,32,8,1,2,32]{5,4,2,1,0,3:T(2,128)} reshape(f32[1024,512]{1,0:T(8,128)S(1)} %fusion.16) | data formatting | bytes 4194304 | tf_op jit(solution)/shard_map/reshape | solution.py:45
  354.9 14.2 %copy.94 = f32[32,32,8,1,2,32]{0,5,1,4,2,3:T(8,128)} copy(f32[32,32,8,1,2,32]{5,4,2,1,0,3:T(2,128)} %reshape.1424) | data formatting | bytes 4194304 | tf_op jit(solution)/shard_map/reshape | solution.py:45
  369.2 11.5 %fusion.8 = (f32[32,32,8,1,2,32]{1,0,5,4,2,3:T(8,128)}, f32[8,1,2,32,32,32]{4,3,5,2,0,1:T(8,128)}) fusion(f32[32,32,8,1,2,32]{0,5,1,4,2,3:T(8,128)} %copy.94, f32[32]{0:T(128)S(1)} %convert_element_type.123, f32[32]{0:T(128)S(1)} %convert_element_type.122, f32[32]{0:T(128)S(1)} %convert_element_type.121, f32[8]{0:T(128)S(1)} %convert_element_type.120), kind=kLoop, calls=%fused_computation.16 | loop fusion | flops 2097152 | bytes 6291872 | tf_op jit(solution)/shard_map/mul | solution.py:103
  396.1 7.7 %reshape.1425 = f32[1024,512]{0,1:T(8,128)} reshape(f32[32,32,8,1,2,32]{1,0,5,4,2,3:T(8,128)} %get-tuple-element.21) | data formatting | bytes 4194304 | tf_op jit(solution)/shard_map/reshape | solution.py:43
  403.8 8.8 %fusion.9 = f32[1024,512]{1,0:T(8,128)S(1)} fusion(f32[1024,512]{0,1:T(8,128)S(1)} %reshape.1426, f32[3,2,1024,1024]{3,2,1,0:T(8,128)} %all-gather.2.cloned.1.call-done, s32[]{:T(128)S(6)} %select_n.50, s32[]{:T(128)S(6)} %add.87), kind=kOutput, calls=%fused_computation.19 | convolution fusion | flops 6442450944 | bytes 8388616 | tf_op jit(solution)/shard_map/dot_general | solution.py:59
  412.6 9.1 %fusion.15 = f32[1024,512]{1,0:T(8,128)S(1)} fusion(f32[1024,512]{1,0:T(8,128)S(1)} %fusion.9, f32[1024,512]{0,1:T(8,128)S(1)} %copy-done.4, f32[3,2,1024,1024]{3,2,1,0:T(8,128)} %all-gather.2.cloned.1.call-done, s32[]{:T(128)S(6)} %select_n.50), kind=kOutput, calls=%fused_computation.32 | convolution fusion | flops 6442975232 | bytes 10485764 | tf_op jit(solution)/shard_map/dot_general | solution.py:57
  421.7 8.3 %reshape.1434 = f32[32,32,8,1,2,32]{5,4,2,1,0,3:T(2,128)} reshape(f32[1024,512]{1,0:T(8,128)S(1)} %fusion.15) | data formatting | bytes 4194304 | tf_op jit(solution)/shard_map/reshape | solution.py:45
  430.0 8.2 %fusion.3 = f32[8,2,32,32,32]{4,0,1,3,2:T(8,128)} fusion(f32[32,32,8,1,2,32]{5,4,2,1,0,3:T(2,128)} %reshape.1434, f32[32]{0:T(128)S(1)} %convert_element_type.127, f32[32]{0:T(128)S(1)} %convert_element_type.126, f32[32]{0:T(128)S(1)} %convert_element_type.125, f32[8]{0:T(128)S(1)} %convert_element_type.124), kind=kLoop, calls=%fused_computation.8 | loop fusion | flops 2097152 | bytes 4194720 | tf_op jit(solution)/shard_map/reduce_sum | solution.py:105
  438.3 66.3 %copy.97 = f32[8,2,32,32,32]{1,4,3,2,0:T(8,128)} copy(f32[8,2,32,32,32]{4,0,1,3,2:T(8,128)} %fusion.3) | data formatting | bytes 4194304 | tf_op jit(solution)/shard_map/reduce_sum | solution.py:105
  506.3 37.9 %psum.7 = f32[64,2]{1,0:T(8,128)S(1)} all-reduce(f32[64,2]{1,0:T(8,128)S(1)} %broadcast_multiply_fusion), channel_id=1, replica_groups=mesh['cuts'=8,'grp'=4] {'cuts','grp'}, use_global_device_ids=true, to_apply=%region_16.17 | all-reduce | flops 128 | bytes 1024 | tf_op jit(solution)/shard_map/psum | solution.py:110
  (67 shorter events, 82.9 us)
Async XLA Ops:
  6.5 153.6 %all-gather.2.cloned.1.call-start = ((), (), s32[]{:S(2)}) async-start(), calls=%async_computation.2 | async-start | bytes 28311552 | tf_op jit(solution)/shard_map/all_gather | solution.py:51
  26.6 13.8 %copy-start.7 = (s32[3]{0:T(128)S(1)}, s32[3]{0:T(128)}, u32[]{:S(2)}) copy-start(s32[3]{0:T(128)} %param.8) | copy-start | bytes 40
  33.7 54.5 %all-to-all-start = ((f32[4,1,131072]{2,1,0:T(1,128)}), f32[4,1,131072]{2,1,0:T(1,128)S(1)}, u32[]{:S(2)}, u32[]{:S(2)}) async-start(f32[4,1,131072]{2,1,0:T(1,128)} %reshape.1435), calls=%async_computation | async-start | bytes 4194304 | tf_op jit(solution)/shard_map/all_to_all | solution.py:73
  88.2 1.4 copy-start.2
  115.5 3.2 copy-start
  160.1 9.0 %copy-start.3 = (f32[1024,512]{0,1:T(8,128)S(1)}, f32[1024,512]{0,1:T(8,128)}, u32[]{:S(2)}) copy-start(f32[1024,512]{0,1:T(8,128)} %reshape.1419) | copy-start | bytes 6291460
  197.3 14.5 %copy-start.9 = (s32[6,3]{0,1:T(4,128)S(1)}, s32[6,3]{0,1:T(4,128)}, u32[]{:S(2)}) copy-start(s32[6,3]{0,1:T(4,128)} %param.9) | copy-start | bytes 220
  197.3 14.5 %copy-start.8 = (s32[1,6]{1,0:T(1,128)S(1)}, s32[1,6]{1,0:T(1,128)}, u32[]{:S(2)}) copy-start(s32[1,6]{1,0:T(1,128)} %param.10) | copy-start | bytes 76
  197.3 16.3 %copy-start.6 = (s32[64,20]{0,1:T(8,128)S(1)}, s32[64,20]{0,1:T(8,128)}, u32[]{:S(2)}) copy-start(s32[64,20]{0,1:T(8,128)} %param.11) | copy-start | bytes 15364
  204.4 52.5 %all-to-all-start.1 = ((f32[4,1,131072]{2,1,0:T(1,128)}), f32[4,1,131072]{2,1,0:T(1,128)}, u32[]{:S(2)}, u32[]{:S(2)}) async-start(f32[4,1,131072]{2,1,0:T(1,128)} %reshape.1437), calls=%async_computation.1 | async-start | bytes 4194304 | tf_op jit(solution)/shard_map/all_to_all | solution.py:80
  280.4 5.8 %copy-start.1 = (f32[32,1,2,32,32,8]{4,5,3,2,1,0:T(8,128)S(1)}, f32[32,1,2,32,32,8]{4,5,3,2,1,0:T(8,128)}, u32[]{:S(2)}) copy-start(f32[32,1,2,32,32,8]{4,5,3,2,1,0:T(8,128)} %copy.90) | copy-start | bytes 6291460
  328.8 9.0 %copy-start.5 = (f32[1024,512]{0,1:T(8,128)S(1)}, f32[1024,512]{0,1:T(8,128)}, u32[]{:S(2)}) copy-start(f32[1024,512]{0,1:T(8,128)} %reshape.1422) | copy-start | bytes 6291460
  403.8 8.8 %copy-start.4 = (f32[1024,512]{0,1:T(8,128)S(1)}, f32[1024,512]{0,1:T(8,128)}, u32[]{:S(2)}) copy-start(f32[1024,512]{0,1:T(8,128)} %reshape.1425) | copy-start | bytes 6291460
Sparse Core Ops, SparseCore 0:
  9.2 127.7 all-gather.1
where the time goes:
time: 558 us; the launch traced here: 552 us
  local copies, waits for them, and re-layouts  274 us (49%)
  waiting for transfers between devices  89.2 us (16%)
  other arithmetic  64.8 us (12%)
  matrix products  54.5 us (10%)
  blocking collectives  37.9 us (7%)
  between operations  19.8 us (4%)
  starting transfers between devices  11.4 us (2%)
    reduce_sum x1, local copies, waits for them, and re-layouts, body(): summed = jnp.sum(current, axis=1)  66.3 us
    unnamed x26, local copies, waits for them, and re-layouts  50.1 us
    all_to_all x1, waiting for transfers between devices, body(): lax.all_to_all(current, 'grp', split_axis=5, concat_axis=0, tiled=True)  45.3 us
    all_to_all x1, waiting for transfers between devices, body(): lax.all_to_all(widened, 'grp', split_axis=0, concat_axis=5, tiled=True)  43.2 us
    reshape x6, local copies, waits for them, and re-layouts, local_pair(): outcome = produce(aligned.reshape(in_rows, -1), turned.reshape(in_rows, -1))  43 us
    psum x1, blocking collectives, body(): return lax.psum(picked, ('cuts', 'grp'))  37.9 us
    reshape x4, local copies, waits for them, and re-layouts, local_pair(): outcome = outcome.reshape((extent, extent) + aligned.shape[2:])  35.8 us
    dot_general x3, matrix products, rows_from(): jnp.dot(columns[0], direct, precision=FULL_PRECISION, preferred_element_t...  27.8 us
  transfers between devices with their start and end apart: 3, of which 2 were waited for; matrix products, arithmetic and copies ran while one was open for 17% of the time, Pallas kernels for 0%

commit v1 on v0

v1 whole, which is shorter than its diff:
```python
import jax
import jax.numpy as jnp
from jax import lax
from jax.sharding import PartitionSpec as P

LAYER_KINDS = (0, 1, 2, 3, 2, 3, 0, 1)
PAIR_GROUPS = ((0, 1), (2, 3), (1, 2), (1, 3))
PRECISION = lax.Precision.HIGH


def keep_mask(cut_index, slice_bits, layers, group_id, positions):
    hit = cut_index[:, 1] == group_id
    active = jnp.zeros_like(hit)
    for layer_id in layers:
        active = jnp.logical_or(active, cut_index[:, 0] == layer_id)
    active = jnp.logical_and(active, hit)
    bit_values = jnp.right_shift(positions[:, None], cut_index[None, :, 2]) & 1
    agrees = bit_values[None, :, :] == slice_bits[:, None, :]
    kept = jnp.logical_or(agrees, jnp.logical_not(active)[None, None, :])
    return jnp.all(kept, axis=2).astype(jnp.float32)


def group_digits(bitstrings):
    bits = bitstrings.shape[1] // 4
    weights = jnp.left_shift(jnp.ones((bits,), jnp.int32), jnp.arange(bits, dtype=jnp.int32))
    return [
        jnp.sum(bitstrings[:, k * bits : (k + 1) * bits] * weights, axis=1).astype(jnp.int32)
        for k in range(4)
    ]


def dot(a, b):
    return jnp.dot(a, b, precision=PRECISION, preferred_element_type=jnp.float32)


def make_body(cuts, grps):

    def body(boundary, gate_stack, layer_order, cut_index, slice_bits, bitstrings):
        c = lax.axis_index("cuts")
        m = lax.axis_index("grp")
        n0, _, ext = boundary.shape[:3]
        pair = ext * ext
        rows = gate_stack.shape[2]
        kdim = n0 * ext
        cols = pair // grps
        local_slices = slice_bits.shape[0]
        g = group_digits(bitstrings)
        count = bitstrings.shape[0]

        gate0 = lax.dynamic_index_in_dim(gate_stack, layer_order[0], 0, keepdims=False)
        gate0 = lax.dynamic_slice_in_dim(gate0, m * kdim, kdim, 2)
        start = jnp.moveaxis(boundary, 1, 0).reshape(2, kdim, pair)
        phi = jnp.stack((
            dot(gate0[0], start[0]) - dot(gate0[1], start[1]),
            dot(gate0[0], start[1]) + dot(gate0[1], start[0]),
        ))
        phi = lax.psum_scatter(phi, "grp", scatter_dimension=2, tiled=True)

        gate1 = lax.dynamic_index_in_dim(gate_stack, layer_order[1], 0, keepdims=False)
        gate1 = lax.dynamic_slice_in_dim(gate1, m * cols, cols, 2)
        gate1 = lax.all_gather(gate1, "cuts", axis=1, tiled=True)

        gate2 = lax.dynamic_index_in_dim(gate_stack, layer_order[2], 0, keepdims=False)
        wanted = g[1] * ext + g[2] - rows * c
        inside = jnp.logical_and(wanted >= 0, wanted < rows)
        picked = jnp.take(gate2, jnp.clip(wanted, 0, rows - 1), axis=1) * inside[None, :, None]
        if ext % cuts == 0:
            width, sub = ext // cuts, 1
            chunk = width * ext
            bits = jnp.zeros((2, cuts, local_slices, chunk), jnp.float32)
            bits = bits.at[:, :, :, : slice_bits.shape[1]].set(slice_bits.astype(jnp.float32))
            own = (jnp.arange(cuts) == c).astype(jnp.float32)
            bits = bits[:, :, None] * own[None, None, :, None, None]
            bits = bits.reshape(2, cuts, cuts * local_slices, chunk)
            bits = jnp.moveaxis(bits, 1, 2)
            packed = jnp.concatenate((picked.reshape(2, count, cuts, chunk), bits), axis=1)
            packed = lax.psum_scatter(packed, "cuts", scatter_dimension=2, tiled=True)[:, :, 0]
            gate2 = packed[:, :count].reshape(2, count, width, ext)
            slice_bits = packed[0, count:, : slice_bits.shape[1]].astype(jnp.int32)
            phi = phi.reshape(2, rows // ext, ext, cols)
            phi = lax.all_to_all(phi, "cuts", split_axis=2, concat_axis=1, tiled=True)
        else:
            width, sub = 1, cuts // ext
            slice_bits = lax.all_gather(slice_bits, "cuts", axis=0, tiled=True)
            picked = lax.psum(picked, "cuts").reshape(2, count, ext, ext)
            gate2 = lax.dynamic_slice_in_dim(picked, c // sub, 1, 2)
            phi = lax.all_gather(phi, "cuts", axis=1, tiled=True).reshape(2, ext, ext, cols)
            phi = lax.dynamic_slice_in_dim(phi, c // sub, 1, 2)
        first_i1 = c // sub * width
        cols = cols // sub
        first_col = (m * sub + c % sub) * cols
        if sub > 1:
            phi = lax.dynamic_slice_in_dim(phi, c % sub * cols, cols, 3)
            gate1 = lax.dynamic_slice_in_dim(gate1, c % sub * cols, cols, 2)

        slices = slice_bits.shape[0]
        column = first_col + jnp.arange(cols, dtype=jnp.int32)
        last = jnp.ones((slices, count), jnp.float32)
        for group_id, layers in ((0, (0, 1, 2)), (1, (2,)), (2, (2,)), (3, (1, 2))):
            last = last * keep_mask(cut_index, slice_bits, layers, group_id, g[group_id])
        on_i1 = keep_mask(
            cut_index, slice_bits, (0, 1), 1, first_i1 + jnp.arange(width, dtype=jnp.int32)
        )
        on_i2 = keep_mask(cut_index, slice_bits, (1,), 2, jnp.arange(ext, dtype=jnp.int32))
        on_j = keep_mask(cut_index, slice_bits, (0,), 2, column // ext)
        on_j = on_j * keep_mask(cut_index, slice_bits, (0,), 3, column % ext)

        left = gate2[:, :, None] * on_i2[None, None, :, None, :]
        left_re = jnp.concatenate((left[0], -left[1]), axis=3)
        left_im = jnp.concatenate((left[1], left[0]), axis=3)
        left = jnp.stack((left_re, left_im), axis=1)
        left = left.reshape(count, 2 * slices * width, 2 * ext)
        right = gate1.reshape(2, ext, ext, cols)
        right = jnp.take(jnp.moveaxis(right, 2, 0).reshape(ext, 2 * ext, cols), g[3], axis=0)
        w = lax.dot_general(
            left, right, (((2,), (1,)), ((0,), (0,))),
            precision=PRECISION, preferred_element_type=jnp.float32,
        )
        w = w.reshape(count, 2, slices, width, cols)
        scale = last.T[:, :, None, None] * on_i1[None, :, :, None] * on_j[None, :, None, :]
        w = jnp.sum(w * scale[:, None], axis=2)
        psi = jnp.take(phi, g[0], axis=1)
        real = jnp.sum(w[:, 0] * psi[0] - w[:, 1] * psi[1], axis=(1, 2))
        imag = jnp.sum(w[:, 0] * psi[1] + w[:, 1] * psi[0], axis=(1, 2))
        return lax.psum(jnp.stack((real, imag), axis=1), ("cuts", "grp"))

    return body


def solution(mesh):
    return jax.shard_map(
        make_body(mesh.shape["cuts"], mesh.shape["grp"]),
        mesh=mesh,
        in_specs=(
            P("grp", None, None, None, None),
            P(None, None, "cuts", None),
            P(),
            P(),
            P("cuts", None),
            P(),
        ),
        out_specs=P(),
        check_vma=False,
    )
```

time: 558 us -> 189 us (0.34)
  local copies, waits for them, and re-layouts: 274 us -> 47.6 us
  waiting for transfers between devices: 89.2 us -> 41.9 us
  matrix products: 54.5 us -> 11.2 us
  other arithmetic: 64.8 us -> 24.6 us
  starting transfers between devices: 11.4 us -> 4.31 us
    all_to_all x2 -> x1, waiting for transfers between devices: 88.5 us -> 6.72 us  [body(): phi = lax.all_to_all(phi, 'cuts', split_axis=2, concat_axis=1, tiled=True)]
    reshape x10 -> x3, local copies, waits for them, and re-layouts: 78.8 us -> 11.2 us  [the longest x1 5.17 us: body(): w = w.reshape(count, 2, slices, width, cols)]
    reduce_sum x1 -> x0, local copies, waits for them, and re-layouts: 66.3 us -> none  [body(): summed = jnp.sum(current, axis=1)]
    transpose x5 -> x0, local copies, waits for them, and re-layouts: 52.6 us -> none  [the longest x2 20.6 us: local_pair(): turned = jnp.moveaxis(rotated(current), (first_dim, second_dim), (0, 1))]
    unnamed x26 -> x14, local copies, waits for them, and re-layouts: 50.1 us -> 0.03 us
    dot_general x6 -> x5, matrix products: 54.5 us -> 11.2 us  [the longest x1 6.82 us: body(): lax.dot_general(left, right, (((2,), (1,)), ((0,), (0,))), precision=PREC...]
    reduce_scatter x0 -> x2, waiting for transfers between devices: none -> 26.5 us  [the longest x1 21.4 us: body(): phi = lax.psum_scatter(phi, 'grp', scatter_dimension=2, tiled=True)]
    all_to_all x4 -> x1, local copies, waits for them, and re-layouts: 21.7 us -> 1.05 us  [body(): phi = lax.all_to_all(phi, 'cuts', split_axis=2, concat_axis=1, tiled=True)]
  transfers between devices with their start and end apart: 3 -> 4, of which waited for: 2 -> 4; matrix products, arithmetic and copies ran while one was open for 17% -> 24% of each run, Pallas kernels for 0% -> 0%
where the time goes in v1:
time: 189 us; the launch traced here: 188 us
  local copies, waits for them, and re-layouts  47.6 us (25%)
  waiting for transfers between devices  41.9 us (22%)
  blocking collectives  39.4 us (21%)
  other arithmetic  24.6 us (13%)
  between operations  19.3 us (10%)
  matrix products  11.2 us (6%)
  starting transfers between devices  4.31 us (2%)
    psum x1, blocking collectives, body(): return lax.psum(jnp.stack((real, imag), axis=1), ('cuts', 'grp'))  39.4 us
    reduce_scatter x1, waiting for transfers between devices, body(): phi = lax.psum_scatter(phi, 'grp', scatter_dimension=2, tiled=True)  21.4 us
    all_gather x1, waiting for transfers between devices, body(): gate1 = lax.all_gather(gate1, 'cuts', axis=1, tiled=True)  8.61 us
    slice x1, local copies, waits for them, and re-layouts, body(): start[0]  8.04 us
    dot_general x1, matrix products, body(): lax.dot_general(left, right, (((2,), (1,)), ((0,), (0,))), precision=PREC...  6.82 us
    all_to_all x1, waiting for transfers between devices, body(): phi = lax.all_to_all(phi, 'cuts', split_axis=2, concat_axis=1, tiled=True)  6.72 us
    gather x2, local copies, waits for them, and re-layouts, body(): jnp.take(gate2, jnp.clip(wanted, 0, rows - 1), axis=1)  5.38 us
    reshape x1, local copies, waits for them, and re-layouts, body(): w = w.reshape(count, 2, slices, width, cols)  5.17 us
  transfers between devices with their start and end apart: 4, of which 4 were waited for; matrix products, arithmetic and copies ran while one was open for 24% of the time, Pallas kernels for 0%

profile of v1, /device:TPU:0, one launch (start us, length us, event | category | flops | bytes accessed | tf_op | source)
XLA Modules:
  0.0 188.2 jit_solution(4543324646269653632)
XLA Ops:
  6.5 1.0 multiply_reduce_fusion.1
  8.2 1.4 fusion.29
  11.8 1.8 copy.72
  13.6 3.1 %gather_fusion = f32[64,2,1024]{2,1,0:T(2,128)} fusion(f32[2,128,1024]{2,0,1:T(2,128)} %bitcast.174, s32[1024]{0:T(1024)S(1)} %pad_clamp_fusion.2), kind=kCustom, calls=%fused_computation | custom fusion | bytes 1048832 | tf_op jit(solution)/shard_map/jit(_take)/gather | solution.py:66
  16.8 2.2 %reshape.612 = f32[2,64,8,128]{3,2,0,1:T(8,128)} reshape(f32[2,64,1024]{2,0,1:T(2,128)} %bitcast.177) | data formatting | bytes 1048576 | tf_op jit(solution)/shard_map/jit(_take)/gather | solution.py:66
  19.1 1.2 fusion.6
  20.4 0.9 copy.41
  22.7 8.0 %fusion.28 = (f32[1,8,32,32,32]{4,3,2,0,1:T(8,128)}, f32[1,8,32,32,32]{4,3,2,0,1:T(8,128)}) fusion(f32[2,8,32,32,32]{4,3,2,0,1:T(8,128)} %bitcast.172), kind=kLoop, calls=%fused_computation.123 | loop fusion | bytes 4194304 | tf_op jit(solution)/shard_map/slice | solution.py:54
  30.7 4.6 %squeeze.45 = f32[256,1024]{1,0:T(8,128)} reshape(f32[1,8,32,32,32]{4,3,2,0,1:T(8,128)} %get-tuple-element.32) | data formatting | bytes 2097152 | tf_op jit(solution)/shard_map/squeeze | solution.py:54
  35.3 4.6 %squeeze.43 = f32[256,1024]{1,0:T(8,128)} reshape(f32[1,8,32,32,32]{4,3,2,0,1:T(8,128)} %get-tuple-element.31) | data formatting | bytes 2097152 | tf_op jit(solution)/shard_map/squeeze | solution.py:54
  40.6 1.8 fusion.7
  42.4 1.7 fusion.5
  45.0 1.1 pad_maximum_fusion.1
  53.4 5.1 %reduce-scatter.3.cloned.1.call-done = f32[2,72,1,128]{3,1,0,2:T(8,128)} async-done(((f32[2,72,8,128]{3,1,0,2:T(8,128)}), f32[2,72,1,128]{3,1,0,2:T(8,128)}) %reduce-scatter.3.cloned.1.call-update) | async-done | bytes 73744 | tf_op jit(solution)/shard_map/reduce_scatter | solution.py:77
  58.6 1.0 copy.42
  63.6 1.1 maximum_bitcast_fusion
  64.7 2.0 %pad_maximum_fusion = f32[64,2,8,4,64]{4,3,2,1,0:T(4,128)} fusion(f32[64,1,8,4,64]{4,3,2,1,0:T(4,128)S(1)} %get-tuple-element.36, f32[64,1,8,4,64]{4,3,2,1,0:T(4,128)S(1)} %get-tuple-element.35), kind=kLoop, calls=%fused_computation.6 | loop fusion | flops 262144 | bytes 2097152 | tf_op jit(solution)/shard_map/stack | solution.py:111
  66.8 21.4 %reduce-scatter.5.cloned.1.call-done = f32[2,128,256]{2,1,0:T(8,128)} async-done(((f32[2,128,1024]{2,1,0:T(8,128)}), f32[2,128,256]{2,1,0:T(8,128)}) %reduce-scatter.5.cloned.1.call-update) | async-done | bytes 262160 | tf_op jit(solution)/shard_map/reduce_scatter | solution.py:57
  88.2 1.8 copy.54
  90.1 4.2 %all-to-all-start = ((f32[2,4,32,256]{3,1,0,2:T(4,128)}), f32[2,4,32,256]{3,1,0,2:T(4,128)}, u32[]{:S(2)}, u32[]{:S(2)}) async-start(f32[2,4,32,256]{3,1,0,2:T(4,128)} %copy.54), calls=%async_computation.2 | async-start | bytes 524288 | tf_op jit(solution)/shard_map/all_to_all | solution.py:81
  94.3 1.7 broadcast_multiply_fusion
  96.0 6.7 %all-to-all-done = f32[2,4,32,256]{3,1,0,2:T(4,128)} async-done(((f32[2,4,32,256]{3,1,0,2:T(4,128)}), f32[2,4,32,256]{3,1,0,2:T(4,128)}, u32[]{:S(2)}, u32[]{:S(2)}) %all-to-all-start) | async-done | bytes 262176 | tf_op jit(solution)/shard_map/all_to_all | solution.py:81
  102.7 1.1 copy.56
  103.8 1.8 gather_fusion.2
  105.6 2.0 %select_bitcast_fusion = f32[2,64,4,256]{3,2,0,1:T(4,128)} fusion(f32[64,2,4,256]{3,2,1,0:T(4,128)} %gather_fusion.2, pred[64]{0:T(512)(128)(4,1)S(1)} %copy-done.4), kind=kLoop, calls=%fused_computation.24 | loop fusion | flops 131072 | bytes 1048640 | tf_op jit(solution)/shard_map/jit(_take)/select_n | solution.py:122
  107.6 8.6 %all-gather.3.cloned.1.call-done = f32[1,2,1024,256]{3,2,1,0:T(8,128)} async-done(((f32[1,2,128,256]{3,2,1,0:T(8,128)}), f32[1,2,1024,256]{3,2,1,0:T(8,128)}) %all-gather.3.cloned.1.call-update) | async-done | bytes 2097168 | tf_op jit(solution)/shard_map/all_gather | solution.py:61
  116.2 4.1 %copy.47 = f32[2,32,32,256]{3,1,0,2:T(8,128)} copy(f32[2,32,32,256]{3,2,1,0:T(8,128)} %bitcast.176) | data formatting | bytes 4194304 | tf_op jit(solution)/shard_map/reshape | solution.py:113
  120.4 4.5 %gather_fusion.1 = f32[64,64,256]{2,1,0:T(8,128)} fusion(f32[32,64,256]{2,1,0:T(8,128)} %bitcast.171, s32[1024]{0:T(1024)} %pad_clamp_fusion.1), kind=kCustom, calls=%fused_computation.1 | custom fusion | bytes 8388864 | tf_op jit(solution)/shard_map/jit(_take)/gather | solution.py:114
  124.8 6.8 %fusion = f32[64,64,256]{2,1,0:T(8,128)} fusion(f32[64,64,64]{2,1,0:T(8,128)} %bitcast.173, f32[64,64,256]{2,1,0:T(8,128)} %gather_fusion.1, pred[64]{0:T(512)(128)(4,1)S(1)} %copy-done.5), kind=kOutput, calls=%fused_computation.4 | convolution fusion | flops 403701760 | bytes 9437248 | tf_op jit(solution)/shard_map/dot_general | solution.py:115
  131.6 5.2 %reshape.584 = f32[64,2,8,4,256]{4,3,2,1,0:T(4,128)} reshape(f32[64,64,256]{2,1,0:T(8,128)} %fusion) | data formatting | bytes 8388608 | tf_op jit(solution)/shard_map/reshape | solution.py:119
  136.8 4.9 %multiply_reduce_fusion = f32[64,2,4,256]{3,2,1,0:T(4,128)S(1)} fusion(f32[64,2,8,4,256]{4,3,2,1,0:T(4,128)} %reshape.584, f32[64,8,4,256]{3,2,1,0:T(4,128)} %broadcast_multiply_fusion), kind=kLoop, calls=%fused_computation.3 | loop fusion | flops 1966080 | bytes 6815744 | tf_op jit(solution)/shard_map/reduce_sum | solution.py:121
  142.3 39.4 %psum.7 = f32[64,2]{0,1:T(2,128)} all-reduce(f32[64,2]{0,1:T(2,128)S(1)} %pad_maximum_fusion.3), channel_id=1, replica_groups=mesh['cuts'=8,'grp'=4] {'cuts','grp'}, use_global_device_ids=true, to_apply=%region_17.18 | all-reduce | flops 128 | bytes 1024 | tf_op jit(solution)/shard_map/psum | solution.py:125
  (65 shorter events, 12.0 us)
Async XLA Ops:
  6.5 5.2 %copy-start = (f32[3,2,128,1024]{3,2,1,0:T(8,128)S(1)}, f32[3,2,128,1024]{3,2,1,0:T(8,128)}, u32[]{:S(2)}) copy-start(f32[3,2,128,1024]{3,2,1,0:T(8,128)} %param.9) | copy-start | bytes 9437188
  6.5 52.0 %reduce-scatter.3.cloned.1.call-start = ((), (), s32[]{:S(2)}) async-start(), calls=%async_computation.3 | async-start | bytes 663552 | tf_op jit(solution)/shard_map/reduce_scatter | solution.py:77
  21.3 66.9 %reduce-scatter.5.cloned.1.call-start = ((), (), s32[]{:S(2)}) async-start(), calls=%async_computation.4 | async-start | bytes 1310720 | tf_op jit(solution)/shard_map/reduce_scatter | solution.py:57
  40.6 3.5 %copy-start.2 = (f32[256,1024]{1,0:T(8,128)S(1)}, f32[256,1024]{1,0:T(8,128)}, u32[]{:S(2)}) copy-start(f32[256,1024]{1,0:T(8,128)} %squeeze.43) | copy-start | bytes 3145732
  40.6 4.0 %copy-start.1 = (f32[256,1024]{1,0:T(8,128)S(1)}, f32[256,1024]{1,0:T(8,128)}, u32[]{:S(2)}) copy-start(f32[256,1024]{1,0:T(8,128)} %squeeze.45) | copy-start | bytes 3145732
  44.5 4.4 %copy-start.6 = (s32[6,3]{0,1:T(4,128)S(1)}, s32[6,3]{0,1:T(4,128)}, u32[]{:S(2)}) copy-start(s32[6,3]{0,1:T(4,128)} %param.11) | copy-start | bytes 220
  46.1 70.1 %all-gather.3.cloned.1.call-start = ((), (), s32[]{:S(2)}) async-start(), calls=%async_computation.5 | async-start | bytes 2359296 | tf_op jit(solution)/shard_map/all_gather | solution.py:61
  66.7 38.9 %copy-start.4 = (pred[64]{0:T(512)(128)(4,1)S(1)}, pred[64]{0:T(512)(128)(4,1)}, u32[]{:S(2)}) copy-start(pred[64]{0:T(512)(128)(4,1)} %get-tuple-element.54) | copy-start | bytes 196
  90.1 12.7 %all-to-all-start = ((f32[2,4,32,256]{3,1,0,2:T(4,128)}), f32[2,4,32,256]{3,1,0,2:T(4,128)}, u32[]{:S(2)}, u32[]{:S(2)}) async-start(f32[2,4,32,256]{3,1,0,2:T(4,128)} %copy.54), calls=%async_computation.2 | async-start | bytes 524288 | tf_op jit(solution)/shard_map/all_to_all | solution.py:81
  120.4 4.5 %copy-start.5 = (pred[64]{0:T(512)(128)(4,1)S(1)}, pred[64]{0:T(512)(128)(4,1)}, u32[]{:S(2)}) copy-start(pred[64]{0:T(512)(128)(4,1)} %get-tuple-element.55) | copy-start | bytes 196
  136.8 4.9 %copy-start.3 = (f32[2,64,4,256]{3,2,0,1:T(4,128)S(1)}, f32[2,64,4,256]{3,2,0,1:T(4,128)}, u32[]{:S(2)}) copy-start(f32[2,64,4,256]{3,2,0,1:T(4,128)} %select_bitcast_fusion) | copy-start | bytes 1572868
Sparse Core Ops, SparseCore 0:
  21.5 37.0 reduce-scatter.2
  60.9 27.3 reduce-scatter.4
  90.1 26.0 all-gather.2

commit v2 on v1

--- a/solution.py
+++ b/solution.py
@@ -1,6 +1,10 @@
+import functools
+
 import jax
 import jax.numpy as jnp
 from jax import lax
+from jax.experimental import pallas as pl
+from jax.experimental.pallas import tpu as pltpu
 from jax.sharding import PartitionSpec as P
 
 LAYER_KINDS = (0, 1, 2, 3, 2, 3, 0, 1)
@@ -127,9 +131,321 @@
     return body
 
 
+VMEM = pl.BlockSpec(memory_space=pltpu.VMEM)
+HI = lax.Precision.HIGHEST
+
+
+def split(x):
+    hi = lax.reduce_precision(x, 8, 7)
+    return hi.astype(jnp.bfloat16), (x - hi).astype(jnp.bfloat16)
+
+
+def flip(index, step):
+    return index + step * (1 - 2 * ((index // step) % 2))
+
+
+def greet(cuts, grps):
+    c, m = lax.axis_index("cuts"), lax.axis_index("grp")
+    barrier = pltpu.get_barrier_semaphore()
+    for d in range(1, cuts):
+        pl.semaphore_signal(barrier, inc=1, device_id={"cuts": (c + d) % cuts})
+    for d in range(1, grps):
+        pl.semaphore_signal(barrier, inc=1, device_id={"grp": (m + d) % grps})
+    pl.semaphore_wait(barrier, cuts + grps - 2)
+    return c, m
+
+
+def exchange_kernel(
+    cuts, grps, lh, ll, bh, bl, u1, packed, u1_all, phi_out, u2_out,
+    parts, landed, phis, u2_in,
+    u_send, u_recv, r_send, r_recv, p_send, p_recv, k_send, k_recv, own_sem,
+):
+    c, m = greet(cuts, grps)
+    core, east, north = flip(c, 1), flip(c, 2), flip(c, 4)
+    half = u1.shape[0] // 2
+    low, high = pl.ds(0, half), pl.ds(half, half)
+
+    def send_u1(slot, src, dst, target):
+        return pltpu.make_async_remote_copy(
+            src_ref=src, dst_ref=dst, send_sem=u_send.at[slot], recv_sem=u_recv.at[slot],
+            device_id={"cuts": target},
+        )
+
+    own = pltpu.make_async_copy(u1, u1_all.at[c], own_sem)
+    own.start()
+    east_low = send_u1(0, u1.at[low], u1_all.at[c, low], east)
+    north_high = send_u1(1, u1.at[high], u1_all.at[c, high], north)
+    east_high = send_u1(2, u1.at[high], u1_all.at[c, high], east)
+    north_low = send_u1(3, u1.at[low], u1_all.at[c, low], north)
+    to_core = send_u1(4, u1, u1_all.at[c], core)
+    for copy in (east_low, north_high, east_high, north_low, to_core):
+        copy.start()
+
+    row_copies = []
+    for d in range(1, cuts):
+        to = (c + d) % cuts
+        copy = pltpu.make_async_remote_copy(
+            src_ref=packed.at[to], dst_ref=u2_in.at[d - 1],
+            send_sem=k_send.at[d - 1], recv_sem=k_recv.at[d - 1], device_id={"cuts": to},
+        )
+        row_copies.append(copy)
+
+    cols = parts.shape[2]
+
+    def product(part):
+        at = pl.ds(pl.multiple_of(part * cols, cols), cols)
+        bhi, blo = bh[:, at], bl[:, at]
+        mm = functools.partial(jnp.dot, preferred_element_type=jnp.float32)
+        return mm(lh[...], bhi) + (mm(lh[...], blo) + mm(ll[...], bhi))
+
+    sums = {}
+    for d in sorted(range(1, grps), key=lambda d: -min(d, grps - d)):
+        to = (m + d) % grps
+        parts[d - 1] = product(to)
+        sums[d] = pltpu.make_async_remote_copy(
+            src_ref=parts.at[d - 1], dst_ref=landed.at[d - 1],
+            send_sem=r_send.at[d - 1], recv_sem=r_recv.at[d - 1], device_id={"grp": to},
+        )
+        sums[d].start()
+    total = product(m)
+
+    east_low.wait_recv()
+    on_north = send_u1(5, u1_all.at[east, low], u1_all.at[east, low], north)
+    on_north.start()
+    north_high.wait_recv()
+    on_east = send_u1(6, u1_all.at[north, high], u1_all.at[north, high], east)
+    on_east.start()
+    for copy in row_copies:
+        copy.start()
+    east_high.wait_recv()
+    core_east = send_u1(7, u1_all.at[east], u1_all.at[east], core)
+    core_east.start()
+    north_low.wait_recv()
+    core_north = send_u1(8, u1_all.at[north], u1_all.at[north], core)
+    core_north.start()
+    on_north.wait_recv()
+    on_east.wait_recv()
+    far = flip(east, 4)
+    core_far = send_u1(9, u1_all.at[far], u1_all.at[far], core)
+    core_far.start()
+
+    for d in range(1, grps):
+        sums[d].wait_recv()
+        total = total + landed[d - 1]
+    phis[...] = total.reshape(phis.shape)
+    phi_out[c] = phis[c]
+    turned = []
+    for d in range(1, cuts):
+        to = (c + d) % cuts
+        copy = pltpu.make_async_remote_copy(
+            src_ref=phis.at[to], dst_ref=phi_out.at[c],
+            send_sem=p_send.at[d - 1], recv_sem=p_recv.at[d - 1], device_id={"cuts": to},
+        )
+        copy.start()
+        turned.append(copy)
+
+    rows = packed[c]
+    for d in range(1, cuts):
+        row_copies[d - 1].wait_recv()
+        rows = rows + u2_in[d - 1]
+    u2_out[...] = rows
+    for copy in (to_core, core_east, core_north, core_far):
+        copy.wait_recv()
+    for copy in turned:
+        copy.wait_recv()
+    own.wait()
+    for copy in (
+        east_low, north_high, east_high, north_low, to_core, on_north, on_east,
+        core_east, core_north, core_far, *row_copies, *sums.values(), *turned,
+    ):
+        copy.wait_send()
+
+
+def finish_kernel(
+    cuts, grps, g0, g3, left, u1_all, phi, on_j, out,
+    acc, mine, from_grp, mid, from_cuts, g_send, g_recv, c_send, c_recv,
+):
+    c, m = greet(cuts, grps)
+    count = left.shape[0]
+    slices = on_j.shape[0]
+    tile = phi.shape[1]
+    lanes = 128
+    row = lax.broadcasted_iota(jnp.int32, (tile, 1), 0)
+    sign = jnp.where(row < tile // 2, 1.0, -1.0)
+
+    def one(b, carry):
+        block = u1_all[:, g3[b]]
+        block = block.reshape(block.shape[0] * block.shape[1], block.shape[2])
+        hi = block.astype(jnp.bfloat16)
+        lo = (block - hi.astype(jnp.float32)).astype(jnp.bfloat16)
+        right = jnp.concatenate((hi, hi, lo), axis=0)
+        w = jnp.dot(left[b], right, preferred_element_type=jnp.float32)
+        w = w.reshape(slices, tile, w.shape[1])
+        w = jnp.sum(w * on_j[...][:, None, :], axis=0)
+        psi = phi[g0[b]]
+        turned = jnp.concatenate((psi[tile // 2 :], psi[: tile // 2]), axis=0)
+        real = jnp.sum(w * psi * sign, axis=0, keepdims=True)
+        imag = jnp.sum(w * turned, axis=0, keepdims=True)
+        fold = lambda v: functools.reduce(
+            lambda p, q: p + q, [v[:, k : k + lanes] for k in range(0, v.shape[1], lanes)]
+        )
+        acc[0, pl.ds(b, 1), :] = fold(real)
+        acc[1, pl.ds(b, 1), :] = fold(imag)
+        return carry
+
+    lax.fori_loop(0, count, one, 0)
+    ones = jnp.ones((8, lanes), jnp.float32)
+    add = lambda v: lax.dot_general(
+        ones, v, (((1,), (1,)), ((), ())), precision=HI, preferred_element_type=jnp.float32
+    )
+    mine[...] = jnp.where(
+        lax.broadcasted_iota(jnp.int32, mine.shape, 0) == 0, add(acc[0]), add(acc[1])
+    )
+
+    def everyone(axis, me, size, src, slots, send, recv):
+        slots[me] = src[...]
+        copies = []
+        for d in range(1, size):
+            to = (me + d) % size
+            copy = pltpu.make_async_remote_copy(
+                src_ref=src, dst_ref=slots.at[me],
+                send_sem=send.at[d - 1], recv_sem=recv.at[d - 1], device_id={axis: to},
+            )
+            copy.start()
+            copies.append(copy)
+        for copy in copies:
+            copy.wait()
+        return functools.reduce(lambda p, q: p + q, [slots[k] for k in range(size)])
+
+    mid[...] = everyone("grp", m, grps, mine, from_grp, g_send, g_recv)
+    out[...] = everyone("cuts", c, cuts, mid, from_cuts, c_send, c_recv)
+
+
+def make_fast_body(cuts, grps):
+
+    def body(boundary, gate_stack, layer_order, cut_index, slice_bits, bitstrings):
+        c = lax.axis_index("cuts")
+        m = lax.axis_index("grp")
+        n0, _, ext = boundary.shape[:3]
+        pair = ext * ext
+        rows = gate_stack.shape[2]
+        kdim = n0 * ext
+        cols = pair // grps
+        width = ext // cuts
+        own_rows = rows // ext
+        local_slices = slice_bits.shape[0]
+        slices = cuts * local_slices
+        g = group_digits(bitstrings)
+        count = bitstrings.shape[0]
+        chunk = width * ext
+        f32 = jnp.float32
+
+        gate0 = lax.dynamic_slice(gate_stack, (layer_order[0], 0, 0, m * kdim), (1, 2, rows, kdim))[0]
+        big = jnp.stack((
+            jnp.concatenate((gate0[0], -gate0[1]), axis=1),
+            jnp.concatenate((gate0[1], gate0[0]), axis=1),
+        ))
+        big = big.reshape(2, own_rows, cuts, width, 2 * kdim)
+        big = jnp.transpose(big, (2, 1, 0, 3, 4)).reshape(2 * rows, 2 * kdim)
+        lh, ll = split(big)
+        start = boundary.reshape(n0, 2, ext, pair)
+        start = jnp.moveaxis(start, 1, 0).reshape(2 * kdim, pair)
+        bh, bl = split(start)
+
+        gate1 = lax.dynamic_slice(gate_stack, (layer_order[1], 0, 0, m * cols), (1, 2, rows, cols))[0]
+        gate1 = jnp.transpose(gate1.reshape(2, own_rows, ext, cols), (2, 0, 1, 3))
+        gate1 = gate1.reshape(ext, 2 * own_rows, cols)
+
+        gate2 = lax.dynamic_index_in_dim(gate_stack, layer_order[2], 0, keepdims=False)
+        wanted = g[1] * ext + g[2] - rows * c
+        pick = (wanted[:, None] == jnp.arange(rows)[None, :]).astype(f32)
+        picked = jnp.stack([jnp.dot(pick, gate2[k], precision=HI) for k in (0, 1)])
+        picked = jnp.transpose(picked.reshape(2 * count, cuts, chunk), (1, 0, 2))
+        extra = -(-slices // 8) * 8
+        bits = jnp.zeros((local_slices, chunk), f32).at[:, : slice_bits.shape[1]].set(slice_bits.astype(f32))
+        bits = lax.dynamic_update_slice(jnp.zeros((extra, chunk), f32), bits, (c * local_slices, 0))
+        bits = jnp.broadcast_to(bits, (cuts, extra, chunk))
+        packed = jnp.concatenate((picked, bits), axis=1)
+
+        dma = pltpu.SemaphoreType.DMA
+        u1_all, phi, u2 = pl.pallas_call(
+            functools.partial(exchange_kernel, cuts, grps),
+            out_shape=(
+                jax.ShapeDtypeStruct((cuts,) + gate1.shape, f32),
+                jax.ShapeDtypeStruct((cuts, 2 * rows // cuts, cols), f32),
+                jax.ShapeDtypeStruct(packed.shape[1:], f32),
+            ),
+            in_specs=[VMEM] * 6,
+            out_specs=(VMEM,) * 3,
+            scratch_shapes=[
+                pltpu.VMEM((grps - 1, 2 * rows, cols), f32),
+                pltpu.VMEM((grps - 1, 2 * rows, cols), f32),
+                pltpu.VMEM((cuts, 2 * rows // cuts, cols), f32),
+                pltpu.VMEM((cuts - 1,) + packed.shape[1:], f32),
+                dma((10,)), dma((10,)), dma((grps - 1,)), dma((grps - 1,)),
+                dma((cuts - 1,)), dma((cuts - 1,)), dma((cuts - 1,)), dma((cuts - 1,)), dma,
+            ],
+            compiler_params=pltpu.CompilerParams(
+                collective_id=0, has_side_effects=True, vmem_limit_bytes=48 << 20
+            ),
+            name="exchange",
+        )(lh, ll, bh, bl, gate1, packed)
+
+        slice_bits = u2[2 * count : 2 * count + slices, : slice_bits.shape[1]].astype(jnp.int32)
+        gate2 = u2[: 2 * count].reshape(2, count, width, cuts, own_rows)
+
+        first_i1 = c * width
+        column = m * cols + jnp.arange(cols, dtype=jnp.int32)
+        last = jnp.ones((slices, count), f32)
+        for group_id, layers in ((0, (0, 1, 2)), (1, (2,)), (2, (2,)), (3, (1, 2))):
+            last = last * keep_mask(cut_index, slice_bits, layers, group_id, g[group_id])
+        on_i1 = keep_mask(
+            cut_index, slice_bits, (0, 1), 1, first_i1 + jnp.arange(width, dtype=jnp.int32)
+        )
+        on_i2 = keep_mask(cut_index, slice_bits, (1,), 2, jnp.arange(ext, dtype=jnp.int32))
+        on_i2 = on_i2.reshape(slices, cuts, own_rows)
+        on_j = keep_mask(cut_index, slice_bits, (0,), 2, column // ext)
+        on_j = on_j * keep_mask(cut_index, slice_bits, (0,), 3, column % ext)
+
+        base = jnp.stack((
+            jnp.stack((gate2[0], -gate2[1]), axis=3),
+            jnp.stack((gate2[1], gate2[0]), axis=3),
+        ), axis=1)
+        scale = last.T[:, :, None] * on_i1[None]
+        left = base[:, None] * scale[:, :, None, :, None, None, None]
+        left = left * on_i2[None, :, None, None, :, None, :]
+        left = left.reshape(count, slices * 2 * width, 2 * ext)
+        hi, lo = split(left)
+        left = jnp.concatenate((hi, lo, hi), axis=2)
+
+        smem = pl.BlockSpec(memory_space=pltpu.SMEM)
+        tile = (8, count)
+        out = pl.pallas_call(
+            functools.partial(finish_kernel, cuts, grps),
+            out_shape=jax.ShapeDtypeStruct(tile, f32),
+            in_specs=[smem, smem] + [VMEM] * 4,
+            out_specs=VMEM,
+            scratch_shapes=[
+                pltpu.VMEM((2, count, 128), f32),
+                pltpu.VMEM(tile, f32), pltpu.VMEM((grps,) + tile, f32),
+                pltpu.VMEM(tile, f32), pltpu.VMEM((cuts,) + tile, f32),
+                dma((grps - 1,)), dma((grps - 1,)), dma((cuts - 1,)), dma((cuts - 1,)),
+            ],
+            compiler_params=pltpu.CompilerParams(
+                collective_id=1, has_side_effects=True, vmem_limit_bytes=48 << 20
+            ),
+            name="finish",
+        )(g[0], g[3], left, u1_all, phi.reshape(ext, 2 * width, cols), on_j)
+        return out[:2].T
+
+    return body
+
+
 def solution(mesh):
+    fast = mesh.shape["cuts"] == 8
+    maker = make_fast_body if fast else make_body
     return jax.shard_map(
-        make_body(mesh.shape["cuts"], mesh.shape["grp"]),
+        maker(mesh.shape["cuts"], mesh.shape["grp"]),
         mesh=mesh,
         in_specs=(
             P("grp", None, None, None, None),

time: 189 us -> 90.1 us (0.48)
  Pallas kernels: 0 us -> 54.9 us
  waiting for transfers between devices: 41.9 us -> 0 us
  blocking collectives: 39.4 us -> 0 us
  local copies, waits for them, and re-layouts: 47.6 us -> 20.1 us
  other arithmetic: 24.6 us -> 5.71 us
  between operations: 19.3 us -> 6.08 us
  matrix products: 11.2 us -> 2.77 us
  starting transfers between devices: 4.31 us -> 0 us
    pallas_call x0 -> x2, Pallas kernels: none -> 54.9 us  [the longest x1 29.7 us: body(): pl.pallas_call(functools.partial(exchange_kernel, cuts, grps), out_shape=...]
    psum x1 -> x0, blocking collectives: 39.4 us -> none  [body(): return lax.psum(jnp.stack((real, imag), axis=1), ('cuts', 'grp'))]
    reduce_scatter x2 -> x0, waiting for transfers between devices: 26.5 us -> none  [the longest x1 21.4 us: body(): phi = lax.psum_scatter(phi, 'grp', scatter_dimension=2, tiled=True)]
    gather x4 -> x0, local copies, waits for them, and re-layouts: 11.6 us -> none  [the longest x2 5.38 us: body(): jnp.take(gate2, jnp.clip(wanted, 0, rows - 1), axis=1)]
    squeeze x3 -> x1, local copies, waits for them, and re-layouts: 9.35 us -> 0.13 us  [body(): gate0[1]]
    all_gather x1 -> x0, waiting for transfers between devices: 8.61 us -> none  [body(): gate1 = lax.all_gather(gate1, 'cuts', axis=1, tiled=True)]
    dot_general x5 -> x2, matrix products: 11.2 us -> 2.77 us  [body(): picked = jnp.stack([jnp.dot(pick, gate2[k], precision=HI) for k in (0, 1)])]
    slice x2 -> x5, local copies, waits for them, and re-layouts: 9.47 us -> 2.55 us  [the longest x1 1.36 us: body(): layer_order[2]]
  transfers between devices with their start and end apart: 4 -> 0, of which waited for: 4 -> 0; matrix products, arithmetic and copies ran while one was open for 24% -> 0% of each run, Pallas kernels for 0% -> 0%
where the time goes in v2:
time: 90.1 us; the launch traced here: 89.6 us
  Pallas kernels  54.9 us (61%)
  local copies, waits for them, and re-layouts  20.1 us (22%)
  between operations  6.08 us (7%)
  other arithmetic  5.71 us (6%)
  matrix products  2.77 us (3%)
    pallas_call x1, Pallas kernels, body(): pl.pallas_call(functools.partial(exchange_kernel, cuts, grps), out_shape=...  29.7 us
    pallas_call x1, Pallas kernels, body(): pl.pallas_call(functools.partial(finish_kernel, cuts, grps), out_shape=ja...  25.2 us
    reshape x2, local copies, waits for them, and re-layouts, body(): start = boundary.reshape(n0, 2, ext, pair)  6.78 us
    mul x4, local copies, waits for them, and re-layouts, body(): left = base[:, None] * scale[:, :, None, :, None, None, None]  5 us
    dot_general x2, matrix products, body(): picked = jnp.stack([jnp.dot(pick, gate2[k], precision=HI) for k in (0, 1)])  2.77 us

profile of v2, /device:TPU:0, one launch (start us, length us, event | category | flops | bytes accessed | tf_op | source)
XLA Modules:
  0.0 89.6 jit_solution(16966377027747319431)
XLA Ops:
  0.0 0.9 multiply_reduce_fusion.1
  0.9 1.4 %fusion.17 = (s32[1]{0:T(128)}, s32[1]{0:T(128)}, s32[1]{0:T(128)}) fusion(s32[3]{0:T(128)} %param.10), kind=kLoop, calls=%fused_computation.94 | loop fusion | bytes 24 | tf_op jit(solution)/shard_map/slice | solution.py:359
  4.3 1.0 %constant_dynamic-slice_fusion.2 = (f32[1,1,128,256]{3,2,1,0:T(8,128)S(1)}, f32[1,1,128,256]{3,2,1,0:T(8,128)S(1)}) fusion(f32[3,2,128,1024]{3,2,1,0:T(8,128)} %param.9, s32[]{:T(128)S(6)} %select_n.37, s32[]{:T(128)S(6)} %add.77, s32[]{:T(128)S(6)} %select_n.38), kind=kLoop, calls=%fused_computation.78 | loop fusion | bytes 524300 | tf_op jit(solution)/shard_map/slice | solution.py:345
  5.3 0.1 concatenate.19
  5.5 0.1 squeeze.17
  5.7 0.3 copy.65
  6.1 0.2 reshape.496
  6.3 6.6 %reshape.497 = f32[8,2,32,1024]{3,2,1,0:T(8,128)S(1)} reshape(f32[8,2,32,32,32]{4,3,2,1,0:T(8,128)} %param.8) | data formatting | bytes 4194304 | tf_op jit(solution)/shard_map/reshape | solution.py:351
  13.0 0.1 copy.66
  13.2 0.4 fusion
  15.2 1.0 %constant_dynamic-slice_fusion.1 = f32[1,2,128,256]{3,2,1,0:T(8,128)S(1)} fusion(f32[3,2,128,1024]{3,2,1,0:T(8,128)} %param.9, s32[]{:T(128)S(6)} %select_n.39, s32[]{:T(128)S(6)} %select_n.38), kind=kLoop, calls=%fused_computation.77 | loop fusion | bytes 524296 | tf_op jit(solution)/shard_map/dynamic_slice | solution.py:355
  16.2 0.2 copy.81.u1
  16.4 0.7 compare_reduce_fusion
  17.1 0.7 broadcast_select_fusion
  19.8 1.4 %convolution_bitcast_fusion = f32[1,64,1024]{2,1,0:T(8,128)S(1)} fusion(f32[3,2,128,1024]{3,2,1,0:T(8,128)} %param.9, s32[]{:T(128)S(6)} %select_n.40, s32[]{:T(128)S(6)} %add.77, s32[64]{0:T(128)S(1)} %add_subtract_fusion), kind=kOutput, calls=%fused_computation.8 | convolution fusion | flops 100671488 | bytes 786696 | tf_op jit(solution)/shard_map/dot_general | solution.py:362
  21.2 1.4 %convolution_bitcast_fusion.1 = f32[1,64,1024]{2,1,0:T(8,128)S(1)} fusion(f32[3,2,128,1024]{3,2,1,0:T(8,128)} %param.9, s32[]{:T(128)S(6)} %select_n.40, s32[64]{0:T(128)S(1)} %add_subtract_fusion), kind=kOutput, calls=%fused_computation.9 | convolution fusion | flops 100671488 | bytes 786692 | tf_op jit(solution)/shard_map/dot_general | solution.py:362
  22.7 0.1 copy.82
  22.8 0.1 copy.86
  22.9 29.7 %exchange.1 = (f32[8,32,8,256]{3,2,1,0:T(8,128)S(1)}, f32[8,32,256]{2,1,0:T(8,128)S(1)}, f32[136,128]{1,0:T(8,128)S(1)}) custom-call(bf16[256,512]{1,0:T(8,128)(2,1)S(1)} %get-tuple-element.40.lh, bf16[256,512]{1,0:T(8,128)(2,1)S(1)} %get-tuple-element.39.ll, bf16[512,1024]{1,0:T(8,128)(2,1)S(1)} %get-tuple-element.38.bh, ...), custom_call_target="tpu_custom_call" | custom-call | tf_op jit(solution)/shard_map/exchange/pallas_call | solution.py:371
  52.6 1.3 %copy-done = f32[8,32,8,256]{3,2,1,0:T(8,128)} copy-done((f32[8,32,8,256]{3,2,1,0:T(8,128)}, f32[8,32,8,256]{3,2,1,0:T(8,128)S(1)}, u32[]{:S(2)}) %copy-start) | copy-done | bytes 2097176
  54.4 1.8 %mul.122 = f32[64,8,2,4,8,2,4]{0,6,5,4,3,2,1:T(4,128)} broadcast(f32[64,2,4,8,2,4]{0,5,4,3,2,1:T(4,128)S(1)} %copy.71), dimensions={0,2,3,4,5,6} | broadcast | bytes 1179648 | tf_op jit(solution)/shard_map/mul | solution.py:415
  56.2 3.1 %copy.76 = f32[64,64,64]{2,1,0:T(8,128)S(1)} copy(f32[64,64,64]{0,2,1:T(8,128)} %bitcast.107) | data formatting | bytes 2097152 | tf_op jit(solution)/shard_map/mul | solution.py:415
  59.7 0.1 copy.79
  59.8 0.2 mul.136
  60.0 0.7 mul.137
  60.8 0.1 or_reduce_fusion.7
  61.1 0.1 or_reduce_fusion.3
  61.4 0.8 fusion.1
  62.2 1.0 %pad_maximum_fusion.left = bf16[64,64,192]{2,1,0:T(8,128)(2,1)S(1)} fusion(bf16[64,64,64]{2,1,0:T(8,128)(2,1)S(1)} %get-tuple-element.36, bf16[64,64,64]{2,1,0:T(8,128)(2,1)S(1)} %get-tuple-element.35), kind=kLoop, calls=%fused_computation.6 | loop fusion | flops 4718592 | bytes 2621440 | tf_op jit(solution)/shard_map/concatenate | solution.py:419
  63.4 0.3 copy-done.1
  63.7 25.2 %finish.1 = f32[8,64]{1,0:T(8,128)S(1)} custom-call(s32[64]{0:T(128)S(1)} %get-tuple-element.25.g0, s32[64]{0:T(128)S(1)} %get-tuple-element.24.g3, bf16[64,64,192]{2,1,0:T(8,128)(2,1)S(1)} %pad_maximum_fusion.left, f32[8,32,8,256]{3,2,1,0:T(8,128)S(1)} %copy-done.1, f32[32,8,256]{2,1,0:T(8,128)S(1)} %bitcast.106, f32[8,256]{1,0:T(8,128)S(1)} %convert_select_fusion.on_j), custom_call_target="tpu_custom_call" | custom-call | tf_op jit(solution)/shard_map/finish/pallas_call | solution.py:423
  89.0 0.6 slice_bitcast_fusion
  (46 shorter events, 1.7 us)
Async XLA Ops:
  13.1 4.0 %copy-start.3 = (s32[1,6]{1,0:T(1,128)S(1)}, s32[1,6]{1,0:T(1,128)}, u32[]{:S(2)}) copy-start(s32[1,6]{1,0:T(1,128)} %param.12) | copy-start | bytes 76
  52.6 1.4 %copy-start = (f32[8,32,8,256]{3,2,1,0:T(8,128)}, f32[8,32,8,256]{3,2,1,0:T(8,128)S(1)}, u32[]{:S(2)}) copy-start(f32[8,32,8,256]{3,2,1,0:T(8,128)S(1)} %get-tuple-element.21.u1_all) | copy-start | bytes 6291460
  56.2 3.2 %copy-start.2 = (s32[6,3]{0,1:T(4,128)S(1)}, s32[6,3]{0,1:T(4,128)}, u32[]{:S(2)}) copy-start(s32[6,3]{0,1:T(4,128)} %param.11) | copy-start | bytes 220
  62.1 1.6 %copy-start.1 = (f32[8,32,8,256]{3,2,1,0:T(8,128)S(1)}, f32[8,32,8,256]{3,2,1,0:T(8,128)}, u32[]{:S(2)}) copy-start(f32[8,32,8,256]{3,2,1,0:T(8,128)} %copy-done) | copy-start | bytes 6291460

commit v3 on v2

--- a/solution.py
+++ b/solution.py
@@ -155,10 +155,12 @@
     return c, m
 
 
-def exchange_kernel(
-    cuts, grps, lh, ll, bh, bl, u1, packed, u1_all, phi_out, u2_out,
-    parts, landed, phis, u2_in,
+def whole_kernel(
+    cuts, grps, g0, g3, lh, ll, bh, bl, u1, packed, out,
+    u1_all, phi, base, masks, weight, wt,
+    parts, landed, phis, u2_in, acc, mine, from_grp, mid, from_cuts,
     u_send, u_recv, r_send, r_recv, p_send, p_recv, k_send, k_recv, own_sem,
+    g_send, g_recv, c_send, c_recv,
 ):
     c, m = greet(cuts, grps)
     core, east, north = flip(c, 1), flip(c, 2), flip(c, 4)
@@ -229,71 +231,109 @@
     core_far = send_u1(9, u1_all.at[far], u1_all.at[far], core)
     core_far.start()
 
+
+    lanes = packed.shape[2]
+    tile = phi.shape[1]
+    half_tile = tile // 2
+    count = wt.shape[0]
+    pairs = count // 2
+    picked_rows = pairs * half_tile
+    for d in range(1, cuts):
+        row_copies[d - 1].wait_recv()
+    rows = packed[c, pl.ds(0, picked_rows)]
+    for d in range(1, cuts):
+        rows = rows + u2_in[d - 1, pl.ds(0, picked_rows)]
+    rows = rows.reshape(picked_rows // tile, tile, lanes)
+    lane = lax.broadcasted_iota(jnp.int32, (1, 1, lanes), 2)
+    row = lax.broadcasted_iota(jnp.int32, (1, tile, 1), 1)
+    quarter = lanes // 4
+    even = (lane // quarter) % 2 == 0
+    real_rows = jnp.where(even, rows, -rows)
+    imag_rows = jnp.where(even, pltpu.roll(rows, lanes - quarter, 2), pltpu.roll(rows, quarter, 2))
+    upper = row < half_tile
+    base[:, 0] = jnp.where(upper, real_rows, pltpu.roll(imag_rows, half_tile, 1))
+    base[:, 1] = jnp.where(upper, pltpu.roll(real_rows, half_tile, 1), imag_rows)
+    first = lax.broadcasted_iota(jnp.int32, (1, lanes), 1) < lanes // 2
+    for s in range(cuts):
+        slot = packed.at[c] if s == 0 else u2_in.at[s - 1]
+        mask = slot[pl.ds(picked_rows, tile)]
+        masks[0, s] = jnp.where(first, mask, 0.0)
+        masks[1, s] = jnp.where(first, 0.0, mask)
+        on_b = slot[pl.ds(picked_rows + tile, tile)]
+        on_j = slot[pl.ds(picked_rows + 2 * tile, tile)]
+        column = jnp.transpose(on_b)[:count, 0:1]
+        weight[s] = column * jnp.concatenate(
+            [on_j[k : k + 1] for k in range(weight.shape[2] // lanes)], axis=1
+        )
+
+    for copy in (to_core, core_east, core_north, core_far):
+        copy.wait_recv()
+    own.wait()
+
+    def block_of(b):
+        block = u1_all[:, g3[b]]
+        block = block.reshape(cuts // 2, 2, tile, block.shape[2])
+        one, two = block[:, 0], block[:, 1]
+        one_t, two_t = pltpu.roll(one, half_tile, 1), pltpu.roll(two, half_tile, 1)
+        re, im = jnp.where(upper, one, two_t), jnp.where(upper, one_t, two)
+        both = jnp.concatenate((re, im), axis=0)
+        return both.reshape(cuts * tile, both.shape[2])
+
+    def in_two(x):
+        hi = x.astype(jnp.bfloat16)
+        return hi, (x - hi.astype(jnp.float32)).astype(jnp.bfloat16)
+
+    mm = functools.partial(jnp.dot, preferred_element_type=jnp.float32)
+
+    def apply_rows(p, carry):
+        right = jnp.concatenate((block_of(p), block_of(p + pairs)), axis=0)
+        rhi, rlo = in_two(right)
+        left = base[p // 2, p % 2][None, None] * masks[...]
+        lhi, llo = in_two(left.reshape(2 * cuts * tile, lanes))
+        w = mm(lhi, rhi) + (mm(lhi, rlo) + mm(llo, rhi))
+        w = w.reshape(2, cuts, tile, w.shape[1])
+        for h in range(2):
+            at = p + h * pairs
+            wt[at] = jnp.sum(w[h] * weight[:, pl.ds(at, 1), :], axis=0)
+        return carry
+
+    lax.fori_loop(0, pairs, apply_rows, 0)
+
     for d in range(1, grps):
         sums[d].wait_recv()
         total = total + landed[d - 1]
     phis[...] = total.reshape(phis.shape)
-    phi_out[c] = phis[c]
+    own_rows = phis.shape[1]
+    place = pl.ds(c * own_rows, own_rows)
+    phi[place] = phis[c]
     turned = []
     for d in range(1, cuts):
         to = (c + d) % cuts
         copy = pltpu.make_async_remote_copy(
-            src_ref=phis.at[to], dst_ref=phi_out.at[c],
+            src_ref=phis.at[to], dst_ref=phi.at[place],
             send_sem=p_send.at[d - 1], recv_sem=p_recv.at[d - 1], device_id={"cuts": to},
         )
         copy.start()
         turned.append(copy)
-
-    rows = packed[c]
-    for d in range(1, cuts):
-        row_copies[d - 1].wait_recv()
-        rows = rows + u2_in[d - 1]
-    u2_out[...] = rows
-    for copy in (to_core, core_east, core_north, core_far):
-        copy.wait_recv()
     for copy in turned:
         copy.wait_recv()
-    own.wait()
-    for copy in (
-        east_low, north_high, east_high, north_low, to_core, on_north, on_east,
-        core_east, core_north, core_far, *row_copies, *sums.values(), *turned,
-    ):
-        copy.wait_send()
-
-
-def finish_kernel(
-    cuts, grps, g0, g3, left, u1_all, phi, on_j, out,
-    acc, mine, from_grp, mid, from_cuts, g_send, g_recv, c_send, c_recv,
-):
-    c, m = greet(cuts, grps)
-    count = left.shape[0]
-    slices = on_j.shape[0]
-    tile = phi.shape[1]
-    lanes = 128
-    row = lax.broadcasted_iota(jnp.int32, (tile, 1), 0)
-    sign = jnp.where(row < tile // 2, 1.0, -1.0)
+
+    sign = jnp.where(lax.broadcasted_iota(jnp.int32, (tile, 1), 0) < half_tile, 1.0, -1.0)
+
+    def fold(v):
+        return functools.reduce(
+            lambda p, q: p + q, [v[:, k : k + lanes] for k in range(0, v.shape[1], lanes)]
+        )
 
     def one(b, carry):
-        block = u1_all[:, g3[b]]
-        block = block.reshape(block.shape[0] * block.shape[1], block.shape[2])
-        hi = block.astype(jnp.bfloat16)
-        lo = (block - hi.astype(jnp.float32)).astype(jnp.bfloat16)
-        right = jnp.concatenate((hi, hi, lo), axis=0)
-        w = jnp.dot(left[b], right, preferred_element_type=jnp.float32)
-        w = w.reshape(slices, tile, w.shape[1])
-        w = jnp.sum(w * on_j[...][:, None, :], axis=0)
         psi = phi[g0[b]]
-        turned = jnp.concatenate((psi[tile // 2 :], psi[: tile // 2]), axis=0)
-        real = jnp.sum(w * psi * sign, axis=0, keepdims=True)
-        imag = jnp.sum(w * turned, axis=0, keepdims=True)
-        fold = lambda v: functools.reduce(
-            lambda p, q: p + q, [v[:, k : k + lanes] for k in range(0, v.shape[1], lanes)]
-        )
-        acc[0, pl.ds(b, 1), :] = fold(real)
-        acc[1, pl.ds(b, 1), :] = fold(imag)
+        w = wt[b]
+        swapped = pltpu.roll(psi, half_tile, 0)
+        acc[0, pl.ds(b, 1), :] = jnp.sum(fold(w * psi) * sign, axis=0, keepdims=True)
+        acc[1, pl.ds(b, 1), :] = jnp.sum(fold(w * swapped), axis=0, keepdims=True)
         return carry
 
-    lax.fori_loop(0, count, one, 0)
+    lax.fori_loop(0, count, one, 0, unroll=4)
     ones = jnp.ones((8, lanes), jnp.float32)
     add = lambda v: lax.dot_general(
         ones, v, (((1,), (1,)), ((), ())), precision=HI, preferred_element_type=jnp.float32
@@ -319,6 +359,11 @@
 
     mid[...] = everyone("grp", m, grps, mine, from_grp, g_send, g_recv)
     out[...] = everyone("cuts", c, cuts, mid, from_cuts, c_send, c_recv)
+    for copy in (
+        east_low, north_high, east_high, north_low, to_core, on_north, on_east,
+        core_east, core_north, core_far, *row_copies, *sums.values(), *turned,
+    ):
+        copy.wait_send()
 
 
 def make_fast_body(cuts, grps):
@@ -333,11 +378,8 @@
         cols = pair // grps
         width = ext // cuts
         own_rows = rows // ext
-        local_slices = slice_bits.shape[0]
-        slices = cuts * local_slices
         g = group_digits(bitstrings)
         count = bitstrings.shape[0]
-        chunk = width * ext
         f32 = jnp.float32
 
         gate0 = lax.dynamic_slice(gate_stack, (layer_order[0], 0, 0, m * kdim), (1, 2, rows, kdim))[0]
@@ -360,82 +402,58 @@
         wanted = g[1] * ext + g[2] - rows * c
         pick = (wanted[:, None] == jnp.arange(rows)[None, :]).astype(f32)
         picked = jnp.stack([jnp.dot(pick, gate2[k], precision=HI) for k in (0, 1)])
-        picked = jnp.transpose(picked.reshape(2 * count, cuts, chunk), (1, 0, 2))
-        extra = -(-slices // 8) * 8
-        bits = jnp.zeros((local_slices, chunk), f32).at[:, : slice_bits.shape[1]].set(slice_bits.astype(f32))
-        bits = lax.dynamic_update_slice(jnp.zeros((extra, chunk), f32), bits, (c * local_slices, 0))
-        bits = jnp.broadcast_to(bits, (cuts, extra, chunk))
-        packed = jnp.concatenate((picked, bits), axis=1)
+        picked = picked.reshape(2, 2, count // 2, cuts, width, ext)
+        picked = jnp.transpose(picked, (3, 2, 4, 1, 0, 5)).reshape(cuts, count // 2 * width, 4 * ext)
+
+        column = m * cols + jnp.arange(cols, dtype=jnp.int32)
+        span = jnp.arange(ext, dtype=jnp.int32)
+        tile, lanes = 2 * width, 4 * ext
+        last = jnp.ones((1, count), f32)
+        for group_id, layers in ((0, (0, 1, 2)), (1, (2,)), (2, (2,)), (3, (1, 2))):
+            last = last * keep_mask(cut_index, slice_bits, layers, group_id, g[group_id])
+        on_i1 = keep_mask(cut_index, slice_bits, (0, 1), 1, span)
+        on_i2 = keep_mask(cut_index, slice_bits, (1,), 2, span)
+        on_j = keep_mask(cut_index, slice_bits, (0,), 2, column // ext)
+        on_j = on_j * keep_mask(cut_index, slice_bits, (0,), 3, column % ext)
+        on_rows = jnp.tile(on_i1.reshape(cuts, width), (1, 2))
+        on_rows = on_rows[:, :, None] * jnp.tile(on_i2, (1, 4))[None]
+        on_b = jnp.pad(last, ((0, tile - 1), (0, lanes - count)))
+        on_j = on_j.reshape(cols // lanes, lanes)
+        on_j = jnp.pad(on_j, ((0, tile - on_j.shape[0]), (0, 0)))
+        shared = jnp.broadcast_to(jnp.concatenate((on_b, on_j))[None], (cuts, 2 * tile, lanes))
+        packed = jnp.concatenate((picked, on_rows, shared), axis=1)
 
         dma = pltpu.SemaphoreType.DMA
-        u1_all, phi, u2 = pl.pallas_call(
-            functools.partial(exchange_kernel, cuts, grps),
-            out_shape=(
-                jax.ShapeDtypeStruct((cuts,) + gate1.shape, f32),
-                jax.ShapeDtypeStruct((cuts, 2 * rows // cuts, cols), f32),
-                jax.ShapeDtypeStruct(packed.shape[1:], f32),
-            ),
-            in_specs=[VMEM] * 6,
-            out_specs=(VMEM,) * 3,
+        smem = pl.BlockSpec(memory_space=pltpu.SMEM)
+        small = (8, count)
+        out = pl.pallas_call(
+            functools.partial(whole_kernel, cuts, grps),
+            out_shape=jax.ShapeDtypeStruct(small, f32),
+            in_specs=[smem, smem] + [VMEM] * 6,
+            out_specs=VMEM,
             scratch_shapes=[
+                pltpu.VMEM((cuts,) + gate1.shape, f32),
+                pltpu.VMEM((ext, tile, cols), f32),
+                pltpu.VMEM((count // 4, 2, tile, lanes), f32),
+                pltpu.VMEM((2, cuts, tile, lanes), f32),
+                pltpu.VMEM((cuts, count, cols), f32),
+                pltpu.VMEM((count, tile, cols), f32),
                 pltpu.VMEM((grps - 1, 2 * rows, cols), f32),
                 pltpu.VMEM((grps - 1, 2 * rows, cols), f32),
-                pltpu.VMEM((cuts, 2 * rows // cuts, cols), f32),
+                pltpu.VMEM((cuts, own_rows, tile, cols), f32),
                 pltpu.VMEM((cuts - 1,) + packed.shape[1:], f32),
+                pltpu.VMEM((2, count, lanes), f32),
+                pltpu.VMEM(small, f32), pltpu.VMEM((grps,) + small, f32),
+                pltpu.VMEM(small, f32), pltpu.VMEM((cuts,) + small, f32),
                 dma((10,)), dma((10,)), dma((grps - 1,)), dma((grps - 1,)),
                 dma((cuts - 1,)), dma((cuts - 1,)), dma((cuts - 1,)), dma((cuts - 1,)), dma,
+                dma((grps - 1,)), dma((grps - 1,)), dma((cuts - 1,)), dma((cuts - 1,)),
             ],
             compiler_params=pltpu.CompilerParams(
                 collective_id=0, has_side_effects=True, vmem_limit_bytes=48 << 20
             ),
-            name="exchange",
-        )(lh, ll, bh, bl, gate1, packed)
-
-        slice_bits = u2[2 * count : 2 * count + slices, : slice_bits.shape[1]].astype(jnp.int32)
-        gate2 = u2[: 2 * count].reshape(2, count, width, cuts, own_rows)
-
-        first_i1 = c * width
-        column = m * cols + jnp.arange(cols, dtype=jnp.int32)
-        last = jnp.ones((slices, count), f32)
-        for group_id, layers in ((0, (0, 1, 2)), (1, (2,)), (2, (2,)), (3, (1, 2))):
-            last = last * keep_mask(cut_index, slice_bits, layers, group_id, g[group_id])
-        on_i1 = keep_mask(
-            cut_index, slice_bits, (0, 1), 1, first_i1 + jnp.arange(width, dtype=jnp.int32)
-        )
-        on_i2 = keep_mask(cut_index, slice_bits, (1,), 2, jnp.arange(ext, dtype=jnp.int32))
-        on_i2 = on_i2.reshape(slices, cuts, own_rows)
-        on_j = keep_mask(cut_index, slice_bits, (0,), 2, column // ext)
-        on_j = on_j * keep_mask(cut_index, slice_bits, (0,), 3, column % ext)
-
-        base = jnp.stack((
-            jnp.stack((gate2[0], -gate2[1]), axis=3),
-            jnp.stack((gate2[1], gate2[0]), axis=3),
-        ), axis=1)
-        scale = last.T[:, :, None] * on_i1[None]
-        left = base[:, None] * scale[:, :, None, :, None, None, None]
-        left = left * on_i2[None, :, None, None, :, None, :]
-        left = left.reshape(count, slices * 2 * width, 2 * ext)
-        hi, lo = split(left)
-        left = jnp.concatenate((hi, lo, hi), axis=2)
-
-        smem = pl.BlockSpec(memory_space=pltpu.SMEM)
-        tile = (8, count)
-        out = pl.pallas_call(
-            functools.partial(finish_kernel, cuts, grps),
-            out_shape=jax.ShapeDtypeStruct(tile, f32),
-            in_specs=[smem, smem] + [VMEM] * 4,
-            out_specs=VMEM,
-            scratch_shapes=[
-                pltpu.VMEM((2, count, 128), f32),
-                pltpu.VMEM(tile, f32), pltpu.VMEM((grps,) + tile, f32),
-                pltpu.VMEM(tile, f32), pltpu.VMEM((cuts,) + tile, f32),
-                dma((grps - 1,)), dma((grps - 1,)), dma((cuts - 1,)), dma((cuts - 1,)),
-            ],
-            compiler_params=pltpu.CompilerParams(
-                collective_id=1, has_side_effects=True, vmem_limit_bytes=48 << 20
-            ),
-            name="finish",
-        )(g[0], g[3], left, u1_all, phi.reshape(ext, 2 * width, cols), on_j)
+            name="whole",
+        )(g[0], g[3], lh, ll, bh, bl, gate1, packed)
         return out[:2].T
 
     return body

time: 90.1 us -> 74.1 us (0.82)
  Pallas kernels: 54.9 us -> 42.5 us
  local copies, waits for them, and re-layouts: 20.1 us -> 17.6 us
    pallas_call x2 -> x1, Pallas kernels: 54.9 us -> 42.5 us  [body(): pl.pallas_call(functools.partial(whole_kernel, cuts, grps), out_shape=jax...]
    mul x6 -> x0, local copies, waits for them, and re-layouts: 5.88 us -> none  [the longest x4 5 us: body(): left = base[:, None] * scale[:, :, None, :, None, None, None]]
    reduce_and x4 -> x3, other arithmetic: 0.38 us -> 2.25 us  [keep_mask(): return jnp.all(kept, axis=2).astype(jnp.float32)]
    unnamed x9 -> x0, local copies, waits for them, and re-layouts: 1.79 us -> none
    dot_general x0 -> x3, local copies, waits for them, and re-layouts: none -> 1.66 us  [body(): picked = jnp.stack([jnp.dot(pick, gate2[k], precision=HI) for k in (0, 1)])]
    transpose x0 -> x1, local copies, waits for them, and re-layouts: none -> 1.62 us  [body(): jnp.transpose(picked, (3, 2, 4, 1, 0, 5))]
    another operation x5 -> x0, other arithmetic: 1.6 us -> none
    reshape x1, local copies, waits for them, and re-layouts: 0.1 us -> 1.58 us  [body(): jnp.transpose(picked, (3, 2, 4, 1, 0, 5))]
where the time goes in v3:
time: 74.1 us; the launch traced here: 73.7 us
  Pallas kernels  42.5 us (57%)
  local copies, waits for them, and re-layouts  17.6 us (24%)
  between operations  5.9 us (8%)
  other arithmetic  4.89 us (7%)
  matrix products  2.83 us (4%)
    pallas_call x1, Pallas kernels, body(): pl.pallas_call(functools.partial(whole_kernel, cuts, grps), out_shape=jax...  42.5 us
    reshape x2, local copies, waits for them, and re-layouts, body(): start = boundary.reshape(n0, 2, ext, pair)  6.78 us
    dot_general x2, matrix products, body(): picked = jnp.stack([jnp.dot(pick, gate2[k], precision=HI) for k in (0, 1)])  2.83 us
    reduce_and x3, other arithmetic, keep_mask(): return jnp.all(kept, axis=2).astype(jnp.float32)  2.25 us
    dot_general x3, local copies, waits for them, and re-layouts, body(): picked = jnp.stack([jnp.dot(pick, gate2[k], precision=HI) for k in (0, 1)])  1.66 us
    transpose x1, local copies, waits for them, and re-layouts, body(): jnp.transpose(picked, (3, 2, 4, 1, 0, 5))  1.62 us
    reshape x1, local copies, waits for them, and re-layouts, body(): jnp.transpose(picked, (3, 2, 4, 1, 0, 5))  1.58 us

profile of v3, /device:TPU:0, one launch (start us, length us, event | category | flops | bytes accessed | tf_op | source)
XLA Modules:
  0.0 73.7 jit_solution(14724380945554085633)
XLA Ops:
  0.0 0.7 slice_bitcast_fusion.1
  0.7 0.9 %multiply_reduce_fusion.1 = (s32[64]{0:T(128)S(1)}, s32[64]{0:T(128)S(1)}, s32[64]{0:T(128)S(1)}, s32[64]{0:T(128)S(1)}) fusion(s32[64,20]{0,1:T(8,128)} %param.11, s32[5]{0:T(128)S(1)} %iota_shift-left_fusion), kind=kLoop, calls=%fused_computation.33 | loop fusion | flops 2304 | bytes 6164 | tf_op jit(solution)/shard_map/reduce_sum | solution.py:31
  1.6 0.1 sub.30
  1.7 1.4 %fusion.28 = (s32[1]{0:T(128)}, s32[1]{0:T(128)}, s32[1]{0:T(128)}) fusion(s32[3]{0:T(128)} %param.8), kind=kLoop, calls=%fused_computation.87 | loop fusion | bytes 24 | tf_op jit(solution)/shard_map/slice | solution.py:401
  8.7 0.8 %fusion.24 = (pred[6]{0:T(512)(128)(4,1)S(1)}, pred[6]{0:T(512)(128)(4,1)S(1)}, pred[6]{0:T(512)(128)(4,1)S(1)}, pred[6]{0:T(512)(128)(4,1)S(1)}, pred[6]{0:T(51...) fusion(s32[6,3]{0,1:T(4,128)} %param.9), kind=kLoop, calls=%fused_computation.60 | loop fusion | flops 156 | bytes 96 | tf_op jit(solution)/shard_map/not | solution.py:23
  9.5 0.7 %fusion.9 = (pred[256]{0:T(512)(128)(4,1)S(1)}, pred[256]{0:T(512)(128)(4,1)S(1)}) fusion(s32[256]{0:T(256)S(1)} %get-tuple-element.38, s32[6]{0:T(128)} %bitcast.118, s32[6]{0:T(128)S(1)} %slice_bitcast_fusion.1, pred[6]{0:T(512)(128)(4,1)S(1)} %get-tuple-element.33, pred[6]{0:T(512)(128)(4,1)S(1)} %get-tuple-element.30, s32[256]{0:T(256)S(1)} %get-tuple-element.39), kind=kLoop, calls=%fused_computation.25 | loop fusion | flops 14848 | bytes 2620 | tf_op jit(solution)/shard_map/reduce_and | solution.py:24
  10.3 0.7 %or_reduce_fusion.1 = (pred[32]{0:T(512)(128)(4,1)S(1)}, pred[32]{0:T(512)(128)(4,1)S(1)}) fusion(s32[6]{0:T(128)} %bitcast.119, s32[6]{0:T(128)S(1)} %slice_bitcast_fusion.1, pred[6]{0:T(512)(128)(4,1)S(1)} %get-tuple-element.34, pred[6]{0:T(512)(128)(4,1)S(1)} %get-tuple-element.27), kind=kLoop, calls=%fused_computation.45 | loop fusion | flops 1280 | bytes 124 | tf_op jit(solution)/shard_map/reduce_and | solution.py:24
  11.0 0.8 %fusion.18 = (pred[64]{0:T(512)(128)(4,1)S(1)}, pred[64]{0:T(512)(128)(4,1)S(1)}, pred[64]{0:T(512)(128)(4,1)S(1)}, pred[64]{0:T(512)(128)(4,1)S(1)}) fusion(s32[64]{0:T(128)S(1)} %get-tuple-element.7.g0, s32[6]{0:T(128)} %bitcast.120, s32[6]{0:T(128)S(1)} %slice_bitcast_fusion.1, pred[6]{0:T(512)(128)(4,1)S(1)} %get-tuple-element.29, ...), kind=kLoop, calls=%fused_computation.43 | loop fusion | flops 7424 | bytes 1352 | tf_op jit(solution)/shard_map/reduce_and | solution.py:24
  11.8 0.1 tile.18
  11.9 0.1 reshape.1126
  12.0 0.1 copy.57
  12.2 1.0 %constant_dynamic-slice_fusion.1 = f32[1,2,128,256]{3,2,1,0:T(8,128)S(1)} fusion(f32[3,2,128,1024]{3,2,1,0:T(8,128)} %param.7, s32[]{:T(128)S(6)} %select_n.36, s32[]{:T(128)S(6)} %select_n.35), kind=kLoop, calls=%fused_computation.71 | loop fusion | bytes 524296 | tf_op jit(solution)/shard_map/dynamic_slice | solution.py:397
  13.2 0.2 copy.60.u1
  13.4 1.0 %constant_dynamic-slice_fusion.2 = (f32[1,1,128,256]{3,2,1,0:T(8,128)S(1)}, f32[1,1,128,256]{3,2,1,0:T(8,128)S(1)}) fusion(f32[3,2,128,1024]{3,2,1,0:T(8,128)} %param.7, s32[]{:T(128)S(6)} %select_n.34, s32[]{:T(128)S(6)} %add.63, s32[]{:T(128)S(6)} %select_n.35), kind=kLoop, calls=%fused_computation.72 | loop fusion | bytes 524300 | tf_op jit(solution)/shard_map/slice | solution.py:387
  14.4 0.1 squeeze.15
  14.5 0.1 concatenate.18
  14.8 0.3 copy.51
  15.1 0.2 reshape.1121
  15.3 0.1 fusion.1
  15.4 1.3 %dynamic-slice_bitcast_fusion.1 = (f32[1024,128]{0,1:T(8,128)S(1)}, f32[1024,128]{0,1:T(8,128)S(1)}) fusion(f32[3,2,128,1024]{3,2,1,0:T(8,128)} %param.7, s32[]{:T(128)S(6)} %select_n.37, s32[]{:T(128)S(6)} %add.63), kind=kLoop, calls=%fused_computation.11 | loop fusion | bytes 2097160 | tf_op jit(solution)/shard_map/dot_general | solution.py:404
  16.7 0.2 copy.54
  16.9 1.4 %convolution_bitcast_fusion.1 = f32[1,2,32,8,4,32]{5,2,4,3,1,0:T(8,128)S(1)} fusion(f32[8,4,32,128,1]{3,2,1,0,4:T(8,128)S(1)} %bitcast.115, s32[2,32]{1,0:T(2,128)S(1)} %sub.30), kind=kOutput, calls=%fused_computation.5 | convolution fusion | flops 100671488 | bytes 786688 | tf_op jit(solution)/shard_map/dot_general | solution.py:404
  18.3 0.2 copy.55
  18.5 1.4 %convolution_bitcast_fusion = f32[1,2,32,8,4,32]{5,2,4,3,1,0:T(8,128)S(1)} fusion(f32[8,4,32,128,1]{3,2,1,0,4:T(8,128)S(1)} %bitcast.114, s32[2,32]{1,0:T(2,128)S(1)} %sub.30), kind=kOutput, calls=%fused_computation.4 | convolution fusion | flops 100671488 | bytes 786688 | tf_op jit(solution)/shard_map/dot_general | solution.py:404
  19.9 0.3 maximum_bitcast_fusion
  20.2 1.6 %copy.56 = f32[8,32,4,2,2,32]{5,4,3,2,1,0:T(2,128)S(1)} copy(f32[8,32,4,2,2,32]{5,1,2,0,3,4:T(8,128)S(1)} %maximum_bitcast_fusion) | data formatting | bytes 1048576 | tf_op jit(solution)/shard_map/transpose | solution.py:406
  21.8 1.6 %reshape.1125 = f32[8,128,128]{2,1,0:T(8,128)S(1)} reshape(f32[8,32,4,2,2,32]{5,4,3,2,1,0:T(2,128)S(1)} %copy.56) | data formatting | bytes 1048576 | tf_op jit(solution)/shard_map/reshape | solution.py:406
  23.5 6.6 %reshape.1122 = f32[8,2,32,1024]{3,2,1,0:T(8,128)S(1)} reshape(f32[8,2,32,32,32]{4,3,2,1,0:T(8,128)} %param.6) | data formatting | bytes 4194304 | tf_op jit(solution)/shard_map/reshape | solution.py:393
  30.1 0.1 copy.52
  30.3 0.4 fusion
  30.6 42.5 %whole.1 = f32[8,64]{1,0:T(8,128)S(1)} custom-call(s32[64]{0:T(128)S(1)} %get-tuple-element.7.g0, s32[64]{0:T(128)S(1)} %get-tuple-element.6.g3, bf16[256,512]{1,0:T(8,128)(2,1)S(1)} %get-tuple-element.24.lh, bf16[256,512]{1,0:T(8,128)(2,1)S(1)} %get-tuple-element.23.ll, bf16[512,1024]{1,0:T(8,128)(2,1)S(1)} %get-tuple-element.22.bh, ...), custom_call_target="tpu_custom_call" | custom-call | tf_op jit(solution)/shard_map/whole/pallas_call | solution.py:429
  73.1 0.6 slice_bitcast_fusion
  (17 shorter events, 0.4 us)

commit v4 on v3

--- a/solution.py
+++ b/solution.py
@@ -381,8 +381,12 @@
         g = group_digits(bitstrings)
         count = bitstrings.shape[0]
         f32 = jnp.float32
-
-        gate0 = lax.dynamic_slice(gate_stack, (layer_order[0], 0, 0, m * kdim), (1, 2, rows, kdim))[0]
+        u32 = jnp.uint32
+        order = layer_order.astype(u32)
+        zero = u32(0)
+        spot = m.astype(u32)
+
+        gate0 = lax.dynamic_slice(gate_stack, (order[0], zero, zero, spot * u32(kdim)), (1, 2, rows, kdim))[0]
         big = jnp.stack((
             jnp.concatenate((gate0[0], -gate0[1]), axis=1),
             jnp.concatenate((gate0[1], gate0[0]), axis=1),
@@ -394,27 +398,38 @@
         start = jnp.moveaxis(start, 1, 0).reshape(2 * kdim, pair)
         bh, bl = split(start)
 
-        gate1 = lax.dynamic_slice(gate_stack, (layer_order[1], 0, 0, m * cols), (1, 2, rows, cols))[0]
+        gate1 = lax.dynamic_slice(gate_stack, (order[1], zero, zero, spot * u32(cols)), (1, 2, rows, cols))[0]
         gate1 = jnp.transpose(gate1.reshape(2, own_rows, ext, cols), (2, 0, 1, 3))
         gate1 = gate1.reshape(ext, 2 * own_rows, cols)
 
-        gate2 = lax.dynamic_index_in_dim(gate_stack, layer_order[2], 0, keepdims=False)
+        gate2 = lax.dynamic_slice(gate_stack, (order[2], zero, zero, zero), (1,) + gate_stack.shape[1:])[0]
         wanted = g[1] * ext + g[2] - rows * c
         pick = (wanted[:, None] == jnp.arange(rows)[None, :]).astype(f32)
-        picked = jnp.stack([jnp.dot(pick, gate2[k], precision=HI) for k in (0, 1)])
-        picked = picked.reshape(2, 2, count // 2, cuts, width, ext)
-        picked = jnp.transpose(picked, (3, 2, 4, 1, 0, 5)).reshape(cuts, count // 2 * width, 4 * ext)
+        picked = lax.dot_general(pick, gate2, (((1,), (1,)), ((), ())), precision=HI)
+        picked = picked.reshape(2, count // 2, 2, cuts, width, ext)
+        picked = jnp.transpose(picked, (3, 1, 4, 0, 2, 5)).reshape(cuts, count // 2 * width, 4 * ext)
 
         column = m * cols + jnp.arange(cols, dtype=jnp.int32)
         span = jnp.arange(ext, dtype=jnp.int32)
         tile, lanes = 2 * width, 4 * ext
-        last = jnp.ones((1, count), f32)
-        for group_id, layers in ((0, (0, 1, 2)), (1, (2,)), (2, (2,)), (3, (1, 2))):
-            last = last * keep_mask(cut_index, slice_bits, layers, group_id, g[group_id])
-        on_i1 = keep_mask(cut_index, slice_bits, (0, 1), 1, span)
-        on_i2 = keep_mask(cut_index, slice_bits, (1,), 2, span)
-        on_j = keep_mask(cut_index, slice_bits, (0,), 2, column // ext)
-        on_j = on_j * keep_mask(cut_index, slice_bits, (0,), 3, column % ext)
+        wants = (
+            (0, 7, g[0]), (1, 4, g[1]), (2, 4, g[2]), (3, 6, g[3]), (1, 3, span), (2, 2, span),
+            (2, 1, column // ext), (3, 1, column % ext),
+        )
+        places = jnp.concatenate([place for _, _, place in wants])
+        group_of = jnp.concatenate([jnp.full(p.shape, k, jnp.int32) for k, _, p in wants])
+        layers_of = jnp.concatenate([jnp.full(p.shape, bits, jnp.int32) for _, bits, p in wants])
+        layer, group, bit = (cut_index[:, k : k + 1] for k in range(3))
+        active = (group == group_of[None]) & ((jnp.right_shift(layers_of[None], layer) & 1) == 1)
+        agrees = (jnp.right_shift(places[None], bit) & 1) == slice_bits.reshape(-1, 1)
+        kept = jnp.min(jnp.where(active & ~agrees, 0.0, 1.0), axis=0)
+        pieces, at = [], 0
+        for _, _, place in wants:
+            pieces.append(kept[at : at + place.shape[0]][None])
+            at += place.shape[0]
+        last = pieces[0] * pieces[1] * pieces[2] * pieces[3]
+        on_i1, on_i2 = pieces[4], pieces[5]
+        on_j = pieces[6] * pieces[7]
         on_rows = jnp.tile(on_i1.reshape(cuts, width), (1, 2))
         on_rows = on_rows[:, :, None] * jnp.tile(on_i2, (1, 4))[None]
         on_b = jnp.pad(last, ((0, tile - 1), (0, lanes - count)))

time: 74.1 us -> 67.9 us (0.916)
  between operations: 5.9 us -> 0.16 us
  other arithmetic: 4.89 us -> 3.18 us
  local copies, waits for them, and re-layouts: 17.6 us -> 19 us
    reduce_and x3 -> x0, other arithmetic: 2.25 us -> none  [keep_mask(): return jnp.all(kept, axis=2).astype(jnp.float32)]
    reduce_min x0 -> x1, other arithmetic: none -> 0.81 us  [body(): kept = jnp.min(jnp.where(active & ~agrees, 0.0, 1.0), axis=0)]
    eq x0 -> x1, local copies, waits for them, and re-layouts: none -> 0.8 us  [body(): group == group_of[None]]
    not x1 -> x0, other arithmetic: 0.77 us -> none  [keep_mask(): kept = jnp.logical_or(agrees, jnp.logical_not(active)[None, None, :])]
    dot_general x3 -> x2, local copies, waits for them, and re-layouts: 1.66 us -> 2.27 us  [body(): lax.dot_general(pick, gate2, (((1,), (1,)), ((), ())), precision=HI)]
    dot_general x2 -> x1, matrix products: 2.83 us -> 2.66 us  [body(): lax.dot_general(pick, gate2, (((1,), (1,)), ((), ())), precision=HI)]
where the time goes in v4:
time: 67.9 us; the launch traced here: 67.5 us
  Pallas kernels  42.5 us (63%)
  local copies, waits for them, and re-layouts  19 us (28%)
  other arithmetic  3.18 us (5%)
  matrix products  2.66 us (4%)
    pallas_call x1, Pallas kernels, body(): pl.pallas_call(functools.partial(whole_kernel, cuts, grps), out_shape=jax...  42.5 us
    reshape x2, local copies, waits for them, and re-layouts, body(): start = boundary.reshape(n0, 2, ext, pair)  6.78 us
    dot_general x1, matrix products, body(): lax.dot_general(pick, gate2, (((1,), (1,)), ((), ())), precision=HI)  2.66 us
    dot_general x2, local copies, waits for them, and re-layouts, body(): lax.dot_general(pick, gate2, (((1,), (1,)), ((), ())), precision=HI)  2.27 us
    dynamic_slice x1, local copies, waits for them, and re-layouts, body(): lax.dynamic_slice(gate_stack, (order[1], zero, zero, spot * u32(cols)), (...  1.66 us
    transpose x1, local copies, waits for them, and re-layouts, body(): jnp.transpose(picked, (3, 1, 4, 0, 2, 5))  1.62 us
    reshape x1, local copies, waits for them, and re-layouts, body(): jnp.transpose(picked, (3, 1, 4, 0, 2, 5))  1.59 us
    slice x1, local copies, waits for them, and re-layouts, body(): gate0[1]  1.55 us

profile of v4, /device:TPU:0, one launch (start us, length us, event | category | flops | bytes accessed | tf_op | source)
XLA Modules:
  0.0 67.5 jit_solution(9446937313068755936)
XLA Ops:
  0.0 0.7 convert_element_type.23
  0.7 0.7 fusion.10
  1.3 0.9 %multiply_reduce_fusion = (s32[64]{0:T(128)S(1)}, s32[64]{0:T(128)S(1)}, s32[64]{0:T(128)S(1)}, s32[64]{0:T(128)S(1)}) fusion(s32[64,20]{0,1:T(8,128)} %param.11, s32[5]{0:T(128)S(1)} %iota_shift-left_fusion), kind=kLoop, calls=%fused_computation.23 | loop fusion | flops 2304 | bytes 6164 | tf_op jit(solution)/shard_map/reduce_sum | solution.py:31
  2.2 0.1 sub.29
  2.3 0.8 %slice_bitcast_fusion.3 = (s32[6]{0:T(128)S(1)}, s32[6]{0:T(128)S(1)}, s32[6]{0:T(128)S(1)}) fusion(s32[6,3]{0,1:T(4,128)} %param.9), kind=kLoop, calls=%fused_computation.43 | loop fusion | bytes 144 | tf_op jit(solution)/shard_map/eq | solution.py:423
  3.1 0.1 concatenate.23
  3.2 0.8 %select_reduce_fusion = f32[832]{0:T(1024)S(1)} fusion(s32[6]{0:T(128)} %bitcast.55, s32[6]{0:T(128)S(1)} %get-tuple-element.20, s32[832]{0:T(1024)S(1)} %concatenate.23, s32[6]{0:T(128)S(1)} %get-tuple-element.21, s32[832]{0:T(1024)} %constant.54.clone.1, s32[832]{0:T(1024)} %constant.53.clone.1, s32[6]{0:T(128)S(1)} %get-tuple-element.19), kind=kLoop, calls=%fused_computation.12 | loop fusion | flops 59072 | bytes 13408 | tf_op jit(solution)/shard_map/reduce_min | solution.py:425
  4.0 0.1 multiply_bitcast_fusion.1
  4.2 0.1 fusion.9
  4.2 0.1 tile.20
  4.3 0.1 tile.16
  4.4 0.1 copy.51
  4.5 0.1 copy.52
  4.6 0.1 broadcast_multiply_fusion
  4.7 1.5 %constant_dynamic-slice_fusion.2 = (f32[1,1,128,256]{3,2,1,0:T(8,128)S(1)}, f32[1,1,128,256]{3,2,1,0:T(8,128)S(1)}) fusion(f32[3,2,128,1024]{3,2,1,0:T(8,128)} %param.7, u32[]{:T(128)} %bitcast, u32[]{:T(128)S(6)} %convert, u32[]{:T(128)S(6)} %mul.88), kind=kLoop, calls=%fused_computation.38 | loop fusion | bytes 524300 | tf_op jit(solution)/shard_map/slice | solution.py:391
  6.2 0.1 squeeze.20
  6.4 0.1 concatenate.20
  6.6 0.3 copy.46
  7.0 0.2 reshape.114
  7.2 0.1 fusion.1
  7.2 1.7 %constant_dynamic-slice_fusion.1 = f32[1,2,128,256]{3,2,1,0:T(8,128)S(1)} fusion(f32[3,2,128,1024]{3,2,1,0:T(8,128)} %param.7, u32[]{:T(128)} %bitcast.5, u32[]{:T(128)S(6)} %mul.88), kind=kLoop, calls=%fused_computation.37 | loop fusion | bytes 524296 | tf_op jit(solution)/shard_map/dynamic_slice | solution.py:401
  8.9 0.2 copy.54.u1
  9.1 1.9 %dynamic-slice_bitcast_fusion = f32[2,1024,128]{1,2,0:T(8,128)S(1)} fusion(f32[3,2,128,1024]{3,2,1,0:T(8,128)} %param.7, u32[]{:T(128)} %bitcast.12), kind=kLoop, calls=%fused_computation.4 | loop fusion | bytes 2097156 | tf_op jit(solution)/shard_map/dot_general | solution.py:408
  11.0 0.3 copy.49
  11.3 2.7 %convolution_bitcast_fusion = f32[8,32,4,2,2,32]{5,1,2,0,4,3:T(8,128)S(1)} fusion(f32[2,8,4,32,128,1]{4,3,2,1,0,5:T(8,128)S(1)} %bitcast.52, s32[2,32]{1,0:T(2,128)S(1)} %sub.29), kind=kOutput, calls=%fused_computation.3 | convolution fusion | flops 201334784 | bytes 1573120 | tf_op jit(solution)/shard_map/dot_general | solution.py:408
  14.0 1.6 %copy.50 = f32[8,32,4,2,2,32]{5,4,3,2,1,0:T(2,128)S(1)} copy(f32[8,32,4,2,2,32]{5,1,2,0,4,3:T(8,128)S(1)} %convolution_bitcast_fusion) | data formatting | bytes 1048576 | tf_op jit(solution)/shard_map/transpose | solution.py:410
  15.6 1.6 %reshape.118 = f32[8,128,128]{2,1,0:T(8,128)S(1)} reshape(f32[8,32,4,2,2,32]{5,4,3,2,1,0:T(2,128)S(1)} %copy.50) | data formatting | bytes 1048576 | tf_op jit(solution)/shard_map/reshape | solution.py:410
  17.3 6.6 %reshape.115 = f32[8,2,32,1024]{3,2,1,0:T(8,128)S(1)} reshape(f32[8,2,32,32,32]{4,3,2,1,0:T(8,128)} %param.6) | data formatting | bytes 4194304 | tf_op jit(solution)/shard_map/reshape | solution.py:397
  23.9 0.1 copy.47
  24.1 0.4 fusion
  24.4 42.5 %whole.1 = f32[8,64]{1,0:T(8,128)S(1)} custom-call(s32[64]{0:T(128)S(1)} %get-tuple-element.7.g0, s32[64]{0:T(128)S(1)} %get-tuple-element.6.g3, bf16[256,512]{1,0:T(8,128)(2,1)S(1)} %get-tuple-element.14.lh, bf16[256,512]{1,0:T(8,128)(2,1)S(1)} %get-tuple-element.13.ll, bf16[512,1024]{1,0:T(8,128)(2,1)S(1)} %get-tuple-element.12.bh, ...), custom_call_target="tpu_custom_call" | custom-call | tf_op jit(solution)/shard_map/whole/pallas_call | solution.py:444
  66.9 0.6 slice_bitcast_fusion
  (13 shorter events, 0.3 us)

commit v5 on v4

--- a/solution.py
+++ b/solution.py
@@ -200,15 +200,20 @@
         mm = functools.partial(jnp.dot, preferred_element_type=jnp.float32)
         return mm(lh[...], bhi) + (mm(lh[...], blo) + mm(ll[...], bhi))
 
-    sums = {}
-    for d in sorted(range(1, grps), key=lambda d: -min(d, grps - d)):
-        to = (m + d) % grps
-        parts[d - 1] = product(to)
-        sums[d] = pltpu.make_async_remote_copy(
-            src_ref=parts.at[d - 1], dst_ref=landed.at[d - 1],
-            send_sem=r_send.at[d - 1], recv_sem=r_recv.at[d - 1], device_id={"grp": to},
-        )
-        sums[d].start()
+    near, across = flip(m, 1), flip(m, 2)
+
+    def send_sum(slot, target):
+        return pltpu.make_async_remote_copy(
+            src_ref=parts.at[slot], dst_ref=landed.at[slot],
+            send_sem=r_send.at[slot], recv_sem=r_recv.at[slot], device_id={"grp": target},
+        )
+
+    sums = [send_sum(0, near), send_sum(1, near), send_sum(2, across)]
+    parts[0] = product(flip(near, 2))
+    sums[0].start()
+    parts[1] = product(near)
+    sums[1].start()
+    carried = product(across)
     total = product(m)
 
     east_low.wait_recv()
@@ -219,6 +224,9 @@
     on_east.start()
     for copy in row_copies:
         copy.start()
+    sums[0].wait_recv()
+    parts[2] = carried + landed[0]
+    sums[2].start()
     east_high.wait_recv()
     core_east = send_u1(7, u1_all.at[east], u1_all.at[east], core)
     core_east.start()
@@ -299,9 +307,9 @@
 
     lax.fori_loop(0, pairs, apply_rows, 0)
 
-    for d in range(1, grps):
-        sums[d].wait_recv()
-        total = total + landed[d - 1]
+    for slot in (1, 2):
+        sums[slot].wait_recv()
+        total = total + landed[slot]
     phis[...] = total.reshape(phis.shape)
     own_rows = phis.shape[1]
     place = pl.ds(c * own_rows, own_rows)
@@ -361,7 +369,7 @@
     out[...] = everyone("cuts", c, cuts, mid, from_cuts, c_send, c_recv)
     for copy in (
         east_low, north_high, east_high, north_low, to_core, on_north, on_east,
-        core_east, core_north, core_far, *row_copies, *sums.values(), *turned,
+        core_east, core_north, core_far, *row_copies, *sums, *turned,
     ):
         copy.wait_send()
 
@@ -475,7 +483,7 @@
 
 
 def solution(mesh):
-    fast = mesh.shape["cuts"] == 8
+    fast = mesh.shape["cuts"] == 8 and mesh.shape["grp"] == 4
     maker = make_fast_body if fast else make_body
     return jax.shard_map(
         maker(mesh.shape["cuts"], mesh.shape["grp"]),

time: 67.9 us -> 67.9 us (level)
  no operation moved by 1% of the time
where the time goes in v5:
time: 67.9 us; the launch traced here: 67.5 us
  Pallas kernels  42.4 us (62%)
  local copies, waits for them, and re-layouts  19 us (28%)
  other arithmetic  3.18 us (5%)
  matrix products  2.66 us (4%)
    pallas_call x1, Pallas kernels, body(): pl.pallas_call(functools.partial(whole_kernel, cuts, grps), out_shape=jax...  42.4 us
    reshape x2, local copies, waits for them, and re-layouts, body(): start = boundary.reshape(n0, 2, ext, pair)  6.78 us
    dot_general x1, matrix products, body(): lax.dot_general(pick, gate2, (((1,), (1,)), ((), ())), precision=HI)  2.66 us
    dot_general x2, local copies, waits for them, and re-layouts, body(): lax.dot_general(pick, gate2, (((1,), (1,)), ((), ())), precision=HI)  2.27 us
    dynamic_slice x1, local copies, waits for them, and re-layouts, body(): lax.dynamic_slice(gate_stack, (order[1], zero, zero, spot * u32(cols)), (...  1.66 us
    transpose x1, local copies, waits for them, and re-layouts, body(): jnp.transpose(picked, (3, 1, 4, 0, 2, 5))  1.62 us
    reshape x1, local copies, waits for them, and re-layouts, body(): jnp.transpose(picked, (3, 1, 4, 0, 2, 5))  1.59 us
    slice x1, local copies, waits for them, and re-layouts, body(): gate0[1]  1.55 us

profile of v5, /device:TPU:0, one launch (start us, length us, event | category | flops | bytes accessed | tf_op | source)
XLA Modules:
  0.0 67.5 jit_solution(7540440635592090612)
XLA Ops:
  0.0 0.7 convert_element_type.23
  0.7 0.7 fusion.10
  1.3 0.9 %multiply_reduce_fusion = (s32[64]{0:T(128)S(1)}, s32[64]{0:T(128)S(1)}, s32[64]{0:T(128)S(1)}, s32[64]{0:T(128)S(1)}) fusion(s32[64,20]{0,1:T(8,128)} %param.11, s32[5]{0:T(128)S(1)} %iota_shift-left_fusion), kind=kLoop, calls=%fused_computation.23 | loop fusion | flops 2304 | bytes 6164 | tf_op jit(solution)/shard_map/reduce_sum | solution.py:31
  2.2 0.1 sub.29
  2.3 0.8 %slice_bitcast_fusion.3 = (s32[6]{0:T(128)S(1)}, s32[6]{0:T(128)S(1)}, s32[6]{0:T(128)S(1)}) fusion(s32[6,3]{0,1:T(4,128)} %param.9), kind=kLoop, calls=%fused_computation.43 | loop fusion | bytes 144 | tf_op jit(solution)/shard_map/eq | solution.py:431
  3.1 0.1 concatenate.23
  3.2 0.8 %select_reduce_fusion = f32[832]{0:T(1024)S(1)} fusion(s32[6]{0:T(128)} %bitcast.55, s32[6]{0:T(128)S(1)} %get-tuple-element.20, s32[832]{0:T(1024)S(1)} %concatenate.23, s32[6]{0:T(128)S(1)} %get-tuple-element.21, s32[832]{0:T(1024)} %constant.54.clone.1, s32[832]{0:T(1024)} %constant.53.clone.1, s32[6]{0:T(128)S(1)} %get-tuple-element.19), kind=kLoop, calls=%fused_computation.12 | loop fusion | flops 59072 | bytes 13408 | tf_op jit(solution)/shard_map/reduce_min | solution.py:433
  4.0 0.1 multiply_bitcast_fusion.1
  4.2 0.1 fusion.9
  4.2 0.1 tile.20
  4.3 0.1 tile.16
  4.4 0.1 copy.51
  4.5 0.1 copy.52
  4.6 0.1 broadcast_multiply_fusion
  4.7 1.5 %constant_dynamic-slice_fusion.2 = (f32[1,1,128,256]{3,2,1,0:T(8,128)S(1)}, f32[1,1,128,256]{3,2,1,0:T(8,128)S(1)}) fusion(f32[3,2,128,1024]{3,2,1,0:T(8,128)} %param.7, u32[]{:T(128)} %bitcast, u32[]{:T(128)S(6)} %convert, u32[]{:T(128)S(6)} %mul.88), kind=kLoop, calls=%fused_computation.38 | loop fusion | bytes 524300 | tf_op jit(solution)/shard_map/slice | solution.py:399
  6.2 0.1 squeeze.20
  6.4 0.1 concatenate.20
  6.6 0.3 copy.46
  7.0 0.2 reshape.114
  7.2 0.1 fusion.1
  7.2 1.7 %constant_dynamic-slice_fusion.1 = f32[1,2,128,256]{3,2,1,0:T(8,128)S(1)} fusion(f32[3,2,128,1024]{3,2,1,0:T(8,128)} %param.7, u32[]{:T(128)} %bitcast.5, u32[]{:T(128)S(6)} %mul.88), kind=kLoop, calls=%fused_computation.37 | loop fusion | bytes 524296 | tf_op jit(solution)/shard_map/dynamic_slice | solution.py:409
  8.9 0.2 copy.54.u1
  9.1 1.9 %dynamic-slice_bitcast_fusion = f32[2,1024,128]{1,2,0:T(8,128)S(1)} fusion(f32[3,2,128,1024]{3,2,1,0:T(8,128)} %param.7, u32[]{:T(128)} %bitcast.12), kind=kLoop, calls=%fused_computation.4 | loop fusion | bytes 2097156 | tf_op jit(solution)/shard_map/dot_general | solution.py:416
  11.0 0.3 copy.49
  11.3 2.7 %convolution_bitcast_fusion = f32[8,32,4,2,2,32]{5,1,2,0,4,3:T(8,128)S(1)} fusion(f32[2,8,4,32,128,1]{4,3,2,1,0,5:T(8,128)S(1)} %bitcast.52, s32[2,32]{1,0:T(2,128)S(1)} %sub.29), kind=kOutput, calls=%fused_computation.3 | convolution fusion | flops 201334784 | bytes 1573120 | tf_op jit(solution)/shard_map/dot_general | solution.py:416
  14.0 1.6 %copy.50 = f32[8,32,4,2,2,32]{5,4,3,2,1,0:T(2,128)S(1)} copy(f32[8,32,4,2,2,32]{5,1,2,0,4,3:T(8,128)S(1)} %convolution_bitcast_fusion) | data formatting | bytes 1048576 | tf_op jit(solution)/shard_map/transpose | solution.py:418
  15.6 1.6 %reshape.118 = f32[8,128,128]{2,1,0:T(8,128)S(1)} reshape(f32[8,32,4,2,2,32]{5,4,3,2,1,0:T(2,128)S(1)} %copy.50) | data formatting | bytes 1048576 | tf_op jit(solution)/shard_map/reshape | solution.py:418
  17.3 6.6 %reshape.115 = f32[8,2,32,1024]{3,2,1,0:T(8,128)S(1)} reshape(f32[8,2,32,32,32]{4,3,2,1,0:T(8,128)} %param.6) | data formatting | bytes 4194304 | tf_op jit(solution)/shard_map/reshape | solution.py:405
  23.9 0.1 copy.47
  24.1 0.4 fusion
  24.4 42.4 %whole.1 = f32[8,64]{1,0:T(8,128)S(1)} custom-call(s32[64]{0:T(128)S(1)} %get-tuple-element.7.g0, s32[64]{0:T(128)S(1)} %get-tuple-element.6.g3, bf16[256,512]{1,0:T(8,128)(2,1)S(1)} %get-tuple-element.14.lh, bf16[256,512]{1,0:T(8,128)(2,1)S(1)} %get-tuple-element.13.ll, bf16[512,1024]{1,0:T(8,128)(2,1)S(1)} %get-tuple-element.12.bh, ...), custom_call_target="tpu_custom_call" | custom-call | tf_op jit(solution)/shard_map/whole/pallas_call | solution.py:452
  66.9 0.6 slice_bitcast_fusion
  (13 shorter events, 0.3 us)

commit v6 on v5

--- a/solution.py
+++ b/solution.py
@@ -305,7 +305,7 @@
             wt[at] = jnp.sum(w[h] * weight[:, pl.ds(at, 1), :], axis=0)
         return carry
 
-    lax.fori_loop(0, pairs, apply_rows, 0)
+    lax.fori_loop(0, pairs, apply_rows, 0, unroll=2)
 
     for slot in (1, 2):
         sums[slot].wait_recv()

time: 67.9 us -> 65.5 us (0.965)
  Pallas kernels: 42.4 us -> 40 us
    pallas_call x1, Pallas kernels: 42.4 us -> 40 us  [body(): pl.pallas_call(functools.partial(whole_kernel, cuts, grps), out_shape=jax...]
where the time goes in v6:
time: 65.5 us; the launch traced here: 65.1 us
  Pallas kernels  40 us (61%)
  local copies, waits for them, and re-layouts  19 us (29%)
  other arithmetic  3.18 us (5%)
  matrix products  2.66 us (4%)
    pallas_call x1, Pallas kernels, body(): pl.pallas_call(functools.partial(whole_kernel, cuts, grps), out_shape=jax...  40 us
    reshape x2, local copies, waits for them, and re-layouts, body(): start = boundary.reshape(n0, 2, ext, pair)  6.78 us
    dot_general x1, matrix products, body(): lax.dot_general(pick, gate2, (((1,), (1,)), ((), ())), precision=HI)  2.66 us
    dot_general x2, local copies, waits for them, and re-layouts, body(): lax.dot_general(pick, gate2, (((1,), (1,)), ((), ())), precision=HI)  2.27 us
    dynamic_slice x1, local copies, waits for them, and re-layouts, body(): lax.dynamic_slice(gate_stack, (order[1], zero, zero, spot * u32(cols)), (...  1.66 us
    transpose x1, local copies, waits for them, and re-layouts, body(): jnp.transpose(picked, (3, 1, 4, 0, 2, 5))  1.62 us
    reshape x1, local copies, waits for them, and re-layouts, body(): jnp.transpose(picked, (3, 1, 4, 0, 2, 5))  1.59 us
    slice x1, local copies, waits for them, and re-layouts, body(): gate0[1]  1.55 us

profile of v6, /device:TPU:0, one launch (start us, length us, event | category | flops | bytes accessed | tf_op | source)
XLA Modules:
  0.0 65.1 jit_solution(5542940465688025882)
XLA Ops:
  0.0 0.7 %convert_element_type.23 = u32[3]{0:T(128)S(1)} convert(s32[3]{0:T(128)} %param.8) | non-fusion elementwise | flops 3 | bytes 24 | tf_op jit(solution)/shard_map/convert_element_type | solution.py:393
  0.7 0.7 %fusion.10 = (u32[1]{0:T(128)}, u32[1]{0:T(128)}, u32[1]{0:T(128)}) fusion(u32[3]{0:T(128)S(1)} %convert_element_type.23), kind=kLoop, calls=%fused_computation.48 | loop fusion | bytes 24 | tf_op jit(solution)/shard_map/slice | solution.py:413
  1.3 0.9 %multiply_reduce_fusion = (s32[64]{0:T(128)S(1)}, s32[64]{0:T(128)S(1)}, s32[64]{0:T(128)S(1)}, s32[64]{0:T(128)S(1)}) fusion(s32[64,20]{0,1:T(8,128)} %param.11, s32[5]{0:T(128)S(1)} %iota_shift-left_fusion), kind=kLoop, calls=%fused_computation.23 | loop fusion | flops 2304 | bytes 6164 | tf_op jit(solution)/shard_map/reduce_sum | solution.py:31
  2.2 0.1 sub.29
  2.3 0.8 %slice_bitcast_fusion.3 = (s32[6]{0:T(128)S(1)}, s32[6]{0:T(128)S(1)}, s32[6]{0:T(128)S(1)}) fusion(s32[6,3]{0,1:T(4,128)} %param.9), kind=kLoop, calls=%fused_computation.43 | loop fusion | bytes 144 | tf_op jit(solution)/shard_map/eq | solution.py:431
  3.1 0.1 concatenate.23
  3.2 0.8 %select_reduce_fusion = f32[832]{0:T(1024)S(1)} fusion(s32[6]{0:T(128)} %bitcast.55, s32[6]{0:T(128)S(1)} %get-tuple-element.20, s32[832]{0:T(1024)S(1)} %concatenate.23, s32[6]{0:T(128)S(1)} %get-tuple-element.21, s32[832]{0:T(1024)} %constant.54.clone.1, s32[832]{0:T(1024)} %constant.53.clone.1, s32[6]{0:T(128)S(1)} %get-tuple-element.19), kind=kLoop, calls=%fused_computation.12 | loop fusion | flops 59072 | bytes 13408 | tf_op jit(solution)/shard_map/reduce_min | solution.py:433
  4.0 0.1 multiply_bitcast_fusion.1
  4.2 0.1 fusion.9
  4.2 0.1 tile.20
  4.3 0.1 tile.16
  4.4 0.1 copy.51
  4.5 0.1 copy.52
  4.6 0.1 broadcast_multiply_fusion
  4.7 1.5 %constant_dynamic-slice_fusion.2 = (f32[1,1,128,256]{3,2,1,0:T(8,128)S(1)}, f32[1,1,128,256]{3,2,1,0:T(8,128)S(1)}) fusion(f32[3,2,128,1024]{3,2,1,0:T(8,128)} %param.7, u32[]{:T(128)} %bitcast, u32[]{:T(128)S(6)} %convert, u32[]{:T(128)S(6)} %mul.88), kind=kLoop, calls=%fused_computation.38 | loop fusion | bytes 524300 | tf_op jit(solution)/shard_map/slice | solution.py:399
  6.2 0.1 squeeze.20
  6.4 0.1 concatenate.20
  6.6 0.3 copy.46
  7.0 0.2 reshape.114
  7.2 0.1 fusion.1
  7.2 1.7 %constant_dynamic-slice_fusion.1 = f32[1,2,128,256]{3,2,1,0:T(8,128)S(1)} fusion(f32[3,2,128,1024]{3,2,1,0:T(8,128)} %param.7, u32[]{:T(128)} %bitcast.5, u32[]{:T(128)S(6)} %mul.88), kind=kLoop, calls=%fused_computation.37 | loop fusion | bytes 524296 | tf_op jit(solution)/shard_map/dynamic_slice | solution.py:409
  8.9 0.2 copy.54.u1
  9.1 1.9 %dynamic-slice_bitcast_fusion = f32[2,1024,128]{1,2,0:T(8,128)S(1)} fusion(f32[3,2,128,1024]{3,2,1,0:T(8,128)} %param.7, u32[]{:T(128)} %bitcast.12), kind=kLoop, calls=%fused_computation.4 | loop fusion | bytes 2097156 | tf_op jit(solution)/shard_map/dot_general | solution.py:416
  11.0 0.3 copy.49
  11.3 2.7 %convolution_bitcast_fusion = f32[8,32,4,2,2,32]{5,1,2,0,4,3:T(8,128)S(1)} fusion(f32[2,8,4,32,128,1]{4,3,2,1,0,5:T(8,128)S(1)} %bitcast.52, s32[2,32]{1,0:T(2,128)S(1)} %sub.29), kind=kOutput, calls=%fused_computation.3 | convolution fusion | flops 201334784 | bytes 1573120 | tf_op jit(solution)/shard_map/dot_general | solution.py:416
  14.0 1.6 %copy.50 = f32[8,32,4,2,2,32]{5,4,3,2,1,0:T(2,128)S(1)} copy(f32[8,32,4,2,2,32]{5,1,2,0,4,3:T(8,128)S(1)} %convolution_bitcast_fusion) | data formatting | bytes 1048576 | tf_op jit(solution)/shard_map/transpose | solution.py:418
  15.6 1.6 %reshape.118 = f32[8,128,128]{2,1,0:T(8,128)S(1)} reshape(f32[8,32,4,2,2,32]{5,4,3,2,1,0:T(2,128)S(1)} %copy.50) | data formatting | bytes 1048576 | tf_op jit(solution)/shard_map/reshape | solution.py:418
  17.3 6.6 %reshape.115 = f32[8,2,32,1024]{3,2,1,0:T(8,128)S(1)} reshape(f32[8,2,32,32,32]{4,3,2,1,0:T(8,128)} %param.6) | data formatting | bytes 4194304 | tf_op jit(solution)/shard_map/reshape | solution.py:405
  23.9 0.1 copy.47
  24.1 0.4 fusion
  24.4 40.0 %whole.1 = f32[8,64]{1,0:T(8,128)S(1)} custom-call(s32[64]{0:T(128)S(1)} %get-tuple-element.7.g0, s32[64]{0:T(128)S(1)} %get-tuple-element.6.g3, bf16[256,512]{1,0:T(8,128)(2,1)S(1)} %get-tuple-element.14.lh, bf16[256,512]{1,0:T(8,128)(2,1)S(1)} %get-tuple-element.13.ll, bf16[512,1024]{1,0:T(8,128)(2,1)S(1)} %get-tuple-element.12.bh, ...), custom_call_target="tpu_custom_call" | custom-call | tf_op jit(solution)/shard_map/whole/pallas_call | solution.py:452
  64.5 0.6 slice_bitcast_fusion
  (13 shorter events, 0.3 us)
